TPU v7x, 32 devices: a whole 2x2x4 slice. The times are simulated.
32 devices in a mesh: owner: 8 (over y, x, core), rows: 4 (over z).
Axes of the slice: x: 2, y: 2, z: 4, core: 2. Of those that a mesh axis runs over, the one named last changes fastest.
Arguments:
- w_down: float32 [64, 1408, 2048], P('owner', None, 'rows'), may hold values from -0.21875 to 0.21875
- router_weight: float32 [2048, 64], P('rows', 'owner'), may hold values from -0.125 to 0.125
- router_gain: float32 [2048], P('rows'), may hold values from 0.25 to 1.75
Outputs:
- serve_down: bfloat16 [64, 1408, 2048], P('owner')
- scale_down: float32 [64, 1408], P('owner')
- serve_router: bfloat16 [2048, 64], replicated
All inputs are finite; a program needn't handle non-finite values. Where the computation divides by a largest or mean magnitude, that divisor is 1e-20 or more.
Results may differ from a plain program's by a relative error of at most 0.001.
Values may be sent and summed in bfloat16 or wider, within the bound.
A program may use at most 192 MiB of HBM per device.

v0:
```python
import jax
import jax.numpy as jnp
from jax import lax
from jax.sharding import PartitionSpec as P


def on_device(w_down, router_weight, router_gain):
    scale_down = lax.pmax(jnp.max(jnp.abs(w_down), axis=2), "rows")
    narrow_down = (w_down / jnp.expand_dims(scale_down, 2)).astype(jnp.bfloat16)
    serve_down = lax.all_gather(narrow_down, "rows", axis=2, tiled=True)
    part_router = (router_weight * router_gain[:, None]).astype(jnp.bfloat16)
    row_router = lax.all_gather(part_router, "rows", axis=0, tiled=True)
    serve_router = lax.all_gather(row_router, "owner", axis=1, tiled=True)
    return (serve_down, scale_down, serve_router)


def solution(mesh):
    placed = (P("owner", None, "rows"), P("rows", "owner"), P("rows"))
    return jax.shard_map(
        on_device,
        mesh=mesh,
        in_specs=placed,
        out_specs=(P("owner", None, None), P("owner", None), P()),
        check_vma=False,
    )
```

profile of v0, /device:TPU:0, one launch (start us, length us, event | category | flops | bytes accessed | tf_op | source)
XLA Modules:
  0.0 854.3 jit_solution(13244291543432159922)
XLA Ops:
  7.2 0.0 all-gather.2.cloned.1.call-start
  7.2 8.2 abs_reduce_fusion
  15.4 21.3 %pmax.7 = f32[8,1408]{1,0:T(8,128)S(1)} all-reduce(f32[8,1408]{1,0:T(8,128)S(1)} %abs_reduce_fusion), channel_id=1, replica_groups=mesh['owner'=8,'rows'=4] {'rows'}, use_global_device_ids=true, to_apply=%region_1.0 | all-reduce | flops 11264 | bytes 90112 | tf_op jit(solution)/shard_map/pmax | solution.py:8
  36.7 0.0 copy-start
  36.7 0.0 copy-start.1
  36.7 0.0 copy-start.2
  36.7 13.0 %divide_convert_fusion = bf16[8,1408,512]{2,1,0:T(8,128)(2,1)} fusion(f32[8,1408,512]{2,1,0:T(8,128)} %param.3, f32[8,1408]{1,0:T(8,128)S(1)} %pmax.7), kind=kLoop, calls=%fused_computation | loop fusion | flops 11534336 | bytes 34648064 | tf_op jit(solution)/shard_map/convert_element_type | solution.py:9
  49.8 0.0 all-gather.2.cloned.1.call-update
  49.8 0.0 copy-done
  49.8 0.0 copy-done.1
  49.8 0.0 copy-done.2
  49.8 13.1 %all_gather.10 = bf16[2048,8]{0,1:T(8,128)(2,1)S(1)} all-gather(bf16[512,8]{0,1:T(8,128)(2,1)S(1)} %multiply_convert_fusion), channel_id=1, replica_groups=mesh['owner'=8,'rows'=4] {'rows'}, dimensions={0}, use_global_device_ids=true | all-gather | bytes 40960 | tf_op jit(solution)/shard_map/all_gather | solution.py:12
  63.0 9.3 %all_gather.11 = bf16[2048,64]{0,1:T(8,128)(2,1)S(1)} all-gather(bf16[2048,8]{0,1:T(8,128)(2,1)S(1)} %all_gather.10), channel_id=1, replica_groups=mesh['owner'=8,'rows'=4] {'owner'}, dimensions={1}, use_global_device_ids=true | all-gather | bytes 294912 | tf_op jit(solution)/shard_map/all_gather | solution.py:13
  72.3 743.6 %all-gather.2.cloned.1.call-done = bf16[8,1408,2048]{2,1,0:T(8,128)(2,1)} async-done(((bf16[8,1408,512]{2,1,0:T(8,128)(2,1)}), bf16[8,1408,2048]{2,1,0:T(8,128)(2,1)}) %all-gather.2.cloned.1.call-update) | async-done | bytes 46137360 | tf_op jit(solution)/shard_map/all_gather | solution.py:10
  815.9 30.8 %copy.8 = bf16[8,1408,2048]{2,1,0:T(8,128)(2,1)} copy(bf16[8,1408,2048]{2,1,0:T(8,128)(2,1)} %all-gather.2.cloned.1.call-done) | data formatting | bytes 92274688
  846.7 0.7 copy.9
  (1 shorter events, 0.0 us)
Async XLA Ops:
  7.2 808.7 %all-gather.2.cloned.1.call-start = ((), (), s32[]{:S(2)}) async-start(), calls=%async_computation | async-start | bytes 57671680 | tf_op jit(solution)/shard_map/all_gather | solution.py:10
  36.7 13.1 %copy-start = (f32[8,1408]{1,0:T(8,128)}, f32[8,1408]{1,0:T(8,128)S(1)}, u32[]{:S(2)}) copy-start(f32[8,1408]{1,0:T(8,128)S(1)} %pmax.7) | copy-start | bytes 135172
  36.7 13.1 %copy-start.1 = (f32[512,8]{0,1:T(8,128)S(1)}, f32[512,8]{0,1:T(8,128)}, u32[]{:S(2)}) copy-start(f32[512,8]{0,1:T(8,128)} %param.4) | copy-start | bytes 49156
  36.7 13.1 %copy-start.2 = (f32[512]{0:T(512)S(1)}, f32[512]{0:T(512)}, u32[]{:S(2)}) copy-start(f32[512]{0:T(512)} %param.5) | copy-start | bytes 6148
Sparse Core Ops, SparseCore 0:
  49.9 765.9 all-gather.1
where the time goes:
time: 854 us
  waiting for transfers between devices  744 us (87%)
  blocking collectives  43.7 us (5%)
  local copies, waits for them, and re-layouts  31.6 us (4%)
  other arithmetic  21.3 us (2%)
  between operations  14.1 us (2%)
    all_gather x1, waiting for transfers between devices, on_device(): serve_down = lax.all_gather(narrow_down, 'rows', axis=2, tiled=True)  744 us
    unnamed x8, local copies, waits for them, and re-layouts  31.6 us
    pmax x1, blocking collectives, on_device(): scale_down = lax.pmax(jnp.max(jnp.abs(w_down), axis=2), 'rows')  21.3 us
  transfers between devices with their start and end apart: 1, of which 1 were waited for; matrix products, arithmetic and copies ran while one was open for 0% of the time, Pallas kernels for 0%

commit v1 on v0

v1 whole, which is shorter than its diff:
```python
import functools

import jax
import jax.numpy as jnp
from jax import lax
from jax.experimental import pallas as pl
from jax.experimental.pallas import tpu as pltpu
from jax.sharding import PartitionSpec as P


LANES = 128
TAIL = 384


def tile_max(ref, e, r):
    block = jnp.abs(ref[e, pl.ds(r, LANES), :LANES])
    for c in range(LANES, ref.shape[2], LANES):
        block = jnp.maximum(block, jnp.abs(ref[e, pl.ds(r, LANES), c : c + LANES]))
    return jnp.max(block.T, axis=0, keepdims=True)


def normalise(values, scales):
    per_row = jnp.broadcast_to(scales, (LANES, LANES)).T
    parts = [values[:, c : c + LANES] / per_row for c in range(0, values.shape[1], LANES)]
    return jnp.concatenate(parts, axis=1).astype(jnp.bfloat16)


def head_kernel(sizes, w_hbm, weight_ref, gain_ref, scale_ref, own_ref, table_ref, held, peak, w_sem, peak_send, peak_recv, row_send, row_recv, all_send, all_recv):
    owners, n = sizes
    experts, depth, _ = w_hbm.shape
    me, mine = lax.axis_index("rows"), lax.axis_index("owner")
    loads = [pltpu.make_async_copy(w_hbm.at[e], held.at[e], w_sem.at[e]) for e in range(experts)]
    for load in loads:
        load.start()

    barrier = pltpu.get_barrier_semaphore()
    for k in range(1, n):
        pl.semaphore_signal(barrier, inc=1, device_id={"rows": lax.rem(me + k, n)}, device_id_type=pl.DeviceIdType.MESH)
    for k in range(1, owners):
        pl.semaphore_signal(barrier, inc=1, device_id={"owner": lax.rem(mine + k, owners)}, device_id_type=pl.DeviceIdType.MESH)
    table_ref[mine, me] = (weight_ref[...] * gain_ref[...]).astype(jnp.bfloat16)
    pl.semaphore_wait(barrier, n - 1 + owners - 1)

    def reduce_expert(e):
        loads[e].wait()
        for r in range(0, depth, LANES):
            peak[me, e : e + 1, r : r + LANES] = tile_max(held, e, r)

    def copies(k_range, ref, key, axis, here, size, send, recv):
        return [
            pltpu.make_async_remote_copy(
                src_ref=ref.at[key],
                dst_ref=ref.at[key],
                send_sem=send.at[k],
                recv_sem=recv.at[k],
                device_id={axis: lax.rem(here + k, size)},
                device_id_type=pl.DeviceIdType.MESH,
            )
            for k in k_range
        ]

    half = experts // 2
    reduce_expert(0)
    to_rows = copies(range(1, n), table_ref, (mine, me), "rows", me, n, row_send, row_recv)
    for copy in to_rows:
        copy.start()
    for e in range(1, half + 1):
        reduce_expert(e)
    for copy in to_rows:
        copy.wait()
    to_owners = copies(range(1, owners), table_ref, mine, "owner", mine, owners, all_send, all_recv)
    for copy in to_owners:
        copy.start()
    for e in range(half + 1, experts):
        reduce_expert(e)
    for copy in to_owners:
        copy.wait()
    to_peers = copies(range(1, n), peak, me, "rows", me, n, peak_send, peak_recv)
    for copy in to_peers:
        copy.start()
    for copy in to_peers:
        copy.wait()
    scale = peak[0]
    for k in range(1, n):
        scale = jnp.maximum(scale, peak[k])
    scale_ref[...] = scale
    for r in range(0, depth, LANES):
        own_ref[pl.ds(r, LANES), :] = normalise(held[0, pl.ds(r, LANES), :], scale_ref[0:1, r : r + LANES])


def head(w_down, router_weight, router_gain, owners, n):
    experts, depth, columns = w_down.shape
    width, share = router_weight.shape
    vmem = pl.BlockSpec(memory_space=pltpu.VMEM)
    dma = pltpu.SemaphoreType.DMA
    return pl.pallas_call(
        functools.partial(head_kernel, (owners, n)),
        out_shape=(
            jax.ShapeDtypeStruct((experts, depth), jnp.float32),
            jax.ShapeDtypeStruct((depth, columns), jnp.bfloat16),
            jax.ShapeDtypeStruct((owners, n, share, width), jnp.bfloat16),
        ),
        in_specs=[pl.BlockSpec(memory_space=pl.ANY), vmem, vmem],
        out_specs=(vmem, vmem, vmem),
        scratch_shapes=[
            pltpu.VMEM(w_down.shape, jnp.float32),
            pltpu.VMEM((n, experts, depth), jnp.float32),
            dma((experts,)),
            dma((n,)),
            dma((n,)),
            dma((n,)),
            dma((n,)),
            dma((owners,)),
            dma((owners,)),
        ],
        compiler_params=pltpu.CompilerParams(collective_id=0, has_side_effects=True, vmem_limit_bytes=48 * 2**20),
    )(w_down, router_weight.T, router_gain[None, :])


def norm_kernel(step_rows, w_ref, scale_ref, own_ref):
    for r in range(0, step_rows, LANES):
        own_ref[pl.ds(r, LANES), :] = normalise(w_ref[0, pl.ds(r, LANES), :], scale_ref[0, 0:1, r : r + LANES])


def norm(w_down, scales, e, row, rows):
    columns = w_down.shape[2]
    step_rows = LANES if row else rows
    at = row // step_rows
    return pl.pallas_call(
        functools.partial(norm_kernel, step_rows),
        out_shape=jax.ShapeDtypeStruct((rows, columns), jnp.bfloat16),
        grid=(rows // step_rows,),
        in_specs=[
            pl.BlockSpec((1, step_rows, columns), lambda r: (e, at + r, 0)),
            pl.BlockSpec((1, 1, step_rows), lambda r: (e, 0, at + r)),
        ],
        out_specs=pl.BlockSpec((step_rows, columns), lambda r: (r, 0)),
        cost_estimate=pl.CostEstimate(flops=rows * columns * 8, bytes_accessed=rows * columns * 6, transcendentals=0),
    )(w_down, scales)


def place_kernel(offsets, n, me_ref, *refs):
    out = refs[-1]
    for offset, block in zip(offsets, refs):
        slot = me_ref[0] + offset
        columns = block.shape[1]

        @pl.when((slot >= 0) & (slot < n))
        def _():
            out[0, :, pl.ds(pl.multiple_of(slot * columns, LANES), columns)] = block[...]


def place(me, blocks, serve, shape, e, row):
    rows, columns = blocks[0].shape
    n = shape[2] // columns
    step_rows = LANES if row else (rows // 2 if rows % 32 == 0 else rows)
    at = row // step_rows

    def spec(offset):
        def index(r, me_ref):
            slot = me_ref[0] + offset
            return jnp.where((slot >= 0) & (slot < n), r, 0), 0

        return pl.BlockSpec((step_rows, columns), index)

    first = serve is None
    return pl.pallas_call(
        functools.partial(place_kernel, tuple(blocks), n),
        out_shape=jax.ShapeDtypeStruct(shape, jnp.bfloat16),
        grid_spec=pltpu.PrefetchScalarGridSpec(
            num_scalar_prefetch=1,
            grid=(rows // step_rows,),
            in_specs=[spec(offset) for offset in blocks] + ([] if first else [pl.BlockSpec(memory_space=pl.ANY)]),
            out_specs=pl.BlockSpec((1, step_rows, shape[2]), lambda r, _: (e, at + r, 0)),
        ),
        input_output_aliases={} if first else {1 + len(blocks): 0},
        cost_estimate=pl.CostEstimate(flops=rows * columns * 64, bytes_accessed=rows * columns * 22, transcendentals=0),
    )(me, *blocks.values(), *([] if first else [serve]))


def plan(experts, depth):
    cut = depth - TAIL
    return [(e, 0, depth) for e in range(experts - 1)] + [(experts - 1, 0, cut), (experts - 1, cut, TAIL)]


def on_device(owners, n, w_down, router_weight, router_gain):
    me = lax.axis_index("rows")
    me_array = me.astype(jnp.int32).reshape((1,))
    experts, depth, columns = w_down.shape
    shape = (experts, depth, n * columns)
    scale_down, first, table = head(w_down, router_weight, router_gain, owners, n)
    scales = scale_down[:, None, :]
    chunks = plan(experts, depth)
    held = []
    serve = None
    for at in range(len(chunks) + n - 1):
        if at < len(chunks):
            held.append({0: first if at == 0 else norm(w_down, scales, *chunks[at])})
        for step in range(1, n):
            c = at - step + 1
            if 0 <= c < len(chunks):
                held[c][-step] = lax.ppermute(held[c][1 - step], "rows", [(i, i + 1) for i in range(step - 1, n - 1)])
                held[c][step] = lax.ppermute(held[c][step - 1], "rows", [(i + 1, i) for i in range(0, n - step)])
        c = at - n + 1
        if c >= 0:
            serve = place(me_array, held[c], serve, shape, *chunks[c][:2])
    serve_router = table.transpose(1, 3, 0, 2).reshape(n * table.shape[3], owners * table.shape[2])
    return (serve, scale_down, serve_router)


def solution(mesh):
    owners, n = mesh.shape["owner"], mesh.shape["rows"]
    placed = (P("owner", None, "rows"), P("rows", "owner"), P("rows"))
    return jax.shard_map(
        functools.partial(on_device, owners, n),
        mesh=mesh,
        in_specs=placed,
        out_specs=(P("owner", None, None), P("owner", None), P()),
        check_vma=False,
    )
```

time: 854 us -> 790 us (0.925)
  waiting for transfers between devices: 744 us -> 597 us
  starting transfers between devices: 0.04 us -> 96.3 us
  Pallas kernels: 0 us -> 88.8 us
  blocking collectives: 43.7 us -> 0 us
  local copies, waits for them, and re-layouts: 31.6 us -> 4.48 us
  other arithmetic: 21.3 us -> 0 us
  between operations: 14.1 us -> 1.44 us
    all_gather x1 -> x0, waiting for transfers between devices: 744 us -> none  [on_device(): serve_down = lax.all_gather(narrow_down, 'rows', axis=2, tiled=True)]
    ppermute x0 -> x54, waiting for transfers between devices: none -> 597 us  [the longest x27 567 us: on_device(): lax.ppermute(held[c][step - 1], 'rows', [(i + 1, i) for i in range(0, n -...]
    ppermute x0 -> x54, starting transfers between devices: none -> 96.3 us  [the longest x27 61.4 us: on_device(): lax.ppermute(held[c][1 - step], 'rows', [(i, i + 1) for i in range(step -...]
    pallas_call x0 -> x18, Pallas kernels: none -> 88.8 us  [the longest x9 44.6 us: place(): pl.pallas_call(functools.partial(place_kernel, tuple(blocks), n), out_sha...]
    unnamed x8 -> x82, local copies, waits for them, and re-layouts: 31.6 us -> 3.83 us
    all_gather x2 -> x0, blocking collectives: 22.4 us -> none  [the longest x1 13.1 us: on_device(): row_router = lax.all_gather(part_router, 'rows', axis=0, tiled=True)]
    pmax x1 -> x0, blocking collectives: 21.3 us -> none  [on_device(): scale_down = lax.pmax(jnp.max(jnp.abs(w_down), axis=2), 'rows')]
    convert_element_type x2 -> x0, other arithmetic: 13.1 us -> none  [the longest x1 13 us: on_device(): narrow_down = (w_down / jnp.expand_dims(scale_down, 2)).astype(jnp.bfloat16)]
  transfers between devices with their start and end apart: 1 -> 54, of which waited for: 1 -> 30; matrix products, arithmetic and copies ran while one was open for 0% -> 0% of each run, Pallas kernels for 0% -> 8%
where the time goes in v1:
time: 790 us; the launch traced here: 788 us
  waiting for transfers between devices  597 us (76%)
  starting transfers between devices  96.3 us (12%)
  Pallas kernels  88.8 us (11%)
    ppermute x27, waiting for transfers between devices, on_device(): lax.ppermute(held[c][step - 1], 'rows', [(i + 1, i) for i in range(0, n -...  567 us
    ppermute x27, starting transfers between devices, on_device(): lax.ppermute(held[c][1 - step], 'rows', [(i, i + 1) for i in range(step -...  61.4 us
    pallas_call x9, Pallas kernels, place(): pl.pallas_call(functools.partial(place_kernel, tuple(blocks), n), out_sha...  44.6 us
    ppermute x27, starting transfers between devices, on_device(): lax.ppermute(held[c][step - 1], 'rows', [(i + 1, i) for i in range(0, n -...  34.9 us
    ppermute x27, waiting for transfers between devices, on_device(): lax.ppermute(held[c][1 - step], 'rows', [(i, i + 1) for i in range(step -...  29.8 us
    pallas_call x8, Pallas kernels, norm(): pl.pallas_call(functools.partial(norm_kernel, step_rows), out_shape=jax.S...  24.9 us
    pallas_call x1, Pallas kernels, head(): pl.pallas_call(functools.partial(head_kernel, (owners, n)), out_shape=(ja...  19.3 us
  transfers between devices with their start and end apart: 54, of which 30 were waited for; matrix products, arithmetic and copies ran while one was open for 0% of the time, Pallas kernels for 8%

profile of v1, /device:TPU:0, one launch (start us, length us, event | category | flops | bytes accessed | tf_op | source)
XLA Modules:
  0.0 787.9 jit_solution(2438120132502991181)
XLA Ops:
  2.0 19.3 %shard_map.58 = (f32[8,1408]{1,0:T(8,128)S(1)}, bf16[1408,512]{1,0:T(8,128)(2,1)S(1)}, bf16[8,4,8,512]{3,2,1,0:T(8,128)(2,1)S(1)}) custom-call(f32[8,1408,512]{2,1,0:T(8,128)} %w_ref.15, f32[8,512]{1,0:T(8,128)S(1)} %bitcast.7, f32[1,512]{1,0:T(1,128)S(1)} %bitcast.8), custom_call_target="tpu_custom_call" | custom-call | tf_op jit(solution)/shard_map/pallas_call | solution.py:96
  25.5 3.2 collective-permute-start
  31.5 3.5 collective-permute-start.6
  39.9 7.1 collective-permute-done.1.refs_2_
  48.3 5.8 collective-permute-start.48
  55.4 3.2 shard_map.66.refs_0_
  58.6 14.4 %collective-permute-start.42 = (bf16[1408,512]{1,0:T(8,128)(2,1)}, bf16[1408,512]{1,0:T(8,128)(2,1)}, u32[]{:S(2)}, u32[]{:S(2)}) collective-permute-start(bf16[1408,512]{1,0:T(8,128)(2,1)} %shard_map.66.refs_0_), channel_id=1, source_target_pairs={{0,1},{1,2},{2,3},{4,5},{5,6},{6,7},{8,9},{9,10},{10,11},{12,13},{... | collective-permute-start | bytes 4325384 | tf_op jit(solution)/shard_map/ppermute | solution.py:202
  75.6 3.2 shard_map.65.refs_0_
  78.9 34.5 %collective-permute-done.7.refs_2_ = bf16[1024,512]{1,0:T(8,128)(2,1)} collective-permute-done((bf16[1024,512]{1,0:T(8,128)(2,1)S(1)}, bf16[1024,512]{1,0:T(8,128)(2,1)}, u32[]{:S(2)}, u32[]{:S(2)}) %collective-permute-start.7) | collective-permute-done | bytes 1048608 | tf_op jit(solution)/shard_map/ppermute | solution.py:203
  113.4 3.3 collective-permute-start.36
  121.2 5.7 collective-permute-start.30
  128.2 3.2 shard_map.63.refs_0_
  131.4 12.9 %collective-permute-done.43.refs_2_ = bf16[1408,512]{1,0:T(8,128)(2,1)} collective-permute-done((bf16[1408,512]{1,0:T(8,128)(2,1)}, bf16[1408,512]{1,0:T(8,128)(2,1)}, u32[]{:S(2)}, u32[]{:S(2)}) %collective-permute-start.43) | collective-permute-done | bytes 1441824 | tf_op jit(solution)/shard_map/ppermute | solution.py:203
  144.3 3.3 collective-permute-start.24
  147.6 3.2 shard_map.62.refs_0_
  155.0 20.2 %collective-permute-done.37.refs_2_ = bf16[1408,512]{1,0:T(8,128)(2,1)} collective-permute-done((bf16[1408,512]{1,0:T(8,128)(2,1)}, bf16[1408,512]{1,0:T(8,128)(2,1)}, u32[]{:S(2)}, u32[]{:S(2)}) %collective-permute-start.37) | collective-permute-done | bytes 1441824 | tf_op jit(solution)/shard_map/ppermute | solution.py:203
  175.2 3.3 collective-permute-start.18
  185.8 20.2 %collective-permute-done.31.refs_2_ = bf16[1408,512]{1,0:T(8,128)(2,1)} collective-permute-done((bf16[1408,512]{1,0:T(8,128)(2,1)}, bf16[1408,512]{1,0:T(8,128)(2,1)}, u32[]{:S(2)}, u32[]{:S(2)}) %collective-permute-start.31) | collective-permute-done | bytes 1441824 | tf_op jit(solution)/shard_map/ppermute | solution.py:203
  208.4 7.1 collective-permute-done.24.refs_1_
  216.7 20.2 %collective-permute-done.25.refs_2_ = bf16[1408,512]{1,0:T(8,128)(2,1)} collective-permute-done((bf16[1408,512]{1,0:T(8,128)(2,1)S(1)}, bf16[1408,512]{1,0:T(8,128)(2,1)}, u32[]{:S(2)}, u32[]{:S(2)}) %collective-permute-start.25) | collective-permute-done | bytes 1441824 | tf_op jit(solution)/shard_map/ppermute | solution.py:203
  238.7 7.7 collective-permute-done.18.refs_1_
  247.6 20.1 %collective-permute-done.19.refs_2_ = bf16[1408,512]{1,0:T(8,128)(2,1)S(1)} collective-permute-done((bf16[1408,512]{1,0:T(8,128)(2,1)S(1)}, bf16[1408,512]{1,0:T(8,128)(2,1)S(1)}, u32[]{:S(2)}, u32[]{:S(2)}) %collective-permute-start.19) | collective-permute-done | bytes 1441824 | tf_op jit(solution)/shard_map/ppermute | solution.py:203
  268.5 7.2 collective-permute-done.12.refs_1_
  277.0 21.7 %collective-permute-done.13.refs_2_ = bf16[1408,512]{1,0:T(8,128)(2,1)S(1)} collective-permute-done((bf16[1408,512]{1,0:T(8,128)(2,1)}, bf16[1408,512]{1,0:T(8,128)(2,1)S(1)}, u32[]{:S(2)}, u32[]{:S(2)}) %collective-permute-start.13) | collective-permute-done | bytes 1441824 | tf_op jit(solution)/shard_map/ppermute | solution.py:203
  300.7 20.5 %collective-permute-done.9.refs_4_ = bf16[1024,512]{1,0:T(8,128)(2,1)} collective-permute-done((bf16[1024,512]{1,0:T(8,128)(2,1)}, bf16[1024,512]{1,0:T(8,128)(2,1)}, u32[]{:S(2)}, u32[]{:S(2)}) %collective-permute-start.9) | collective-permute-done | bytes 1048608 | tf_op jit(solution)/shard_map/ppermute | solution.py:203
  323.3 28.7 %collective-permute-done.51.refs_4_ = bf16[1408,512]{1,0:T(8,128)(2,1)S(1)} collective-permute-done((bf16[1408,512]{1,0:T(8,128)(2,1)}, bf16[1408,512]{1,0:T(8,128)(2,1)S(1)}, u32[]{:S(2)}, u32[]{:S(2)}) %collective-permute-start.51) | collective-permute-done | bytes 1441824 | tf_op jit(solution)/shard_map/ppermute | solution.py:203
  354.1 28.8 %collective-permute-done.45.refs_4_ = bf16[1408,512]{1,0:T(8,128)(2,1)S(1)} collective-permute-done((bf16[1408,512]{1,0:T(8,128)(2,1)}, bf16[1408,512]{1,0:T(8,128)(2,1)S(1)}, u32[]{:S(2)}, u32[]{:S(2)}) %collective-permute-start.45) | collective-permute-done | bytes 1441824 | tf_op jit(solution)/shard_map/ppermute | solution.py:203
  385.0 28.8 %collective-permute-done.39.refs_4_ = bf16[1408,512]{1,0:T(8,128)(2,1)S(1)} collective-permute-done((bf16[1408,512]{1,0:T(8,128)(2,1)}, bf16[1408,512]{1,0:T(8,128)(2,1)S(1)}, u32[]{:S(2)}, u32[]{:S(2)}) %collective-permute-start.39) | collective-permute-done | bytes 1441824 | tf_op jit(solution)/shard_map/ppermute | solution.py:203
  415.9 28.8 %collective-permute-done.33.refs_4_ = bf16[1408,512]{1,0:T(8,128)(2,1)S(1)} collective-permute-done((bf16[1408,512]{1,0:T(8,128)(2,1)}, bf16[1408,512]{1,0:T(8,128)(2,1)S(1)}, u32[]{:S(2)}, u32[]{:S(2)}) %collective-permute-start.33) | collective-permute-done | bytes 1441824 | tf_op jit(solution)/shard_map/ppermute | solution.py:203
  446.8 28.8 %collective-permute-done.27.refs_4_ = bf16[1408,512]{1,0:T(8,128)(2,1)S(1)} collective-permute-done((bf16[1408,512]{1,0:T(8,128)(2,1)}, bf16[1408,512]{1,0:T(8,128)(2,1)S(1)}, u32[]{:S(2)}, u32[]{:S(2)}) %collective-permute-start.27) | collective-permute-done | bytes 1441824 | tf_op jit(solution)/shard_map/ppermute | solution.py:203
  477.7 28.8 %collective-permute-done.21.refs_4_ = bf16[1408,512]{1,0:T(8,128)(2,1)S(1)} collective-permute-done((bf16[1408,512]{1,0:T(8,128)(2,1)S(1)}, bf16[1408,512]{1,0:T(8,128)(2,1)S(1)}, u32[]{:S(2)}, u32[]{:S(2)}) %collective-permute-start.21) | collective-permute-done | bytes 1441824 | tf_op jit(solution)/shard_map/ppermute | solution.py:203
  508.6 28.9 %collective-permute-done.15.refs_4_ = bf16[1408,512]{1,0:T(8,128)(2,1)} collective-permute-done((bf16[1408,512]{1,0:T(8,128)(2,1)S(1)}, bf16[1408,512]{1,0:T(8,128)(2,1)}, u32[]{:S(2)}, u32[]{:S(2)}) %collective-permute-start.15) | collective-permute-done | bytes 1441824 | tf_op jit(solution)/shard_map/ppermute | solution.py:203
  539.6 28.7 %collective-permute-done.53.refs_6_ = bf16[1408,512]{1,0:T(8,128)(2,1)S(1)} collective-permute-done((bf16[1408,512]{1,0:T(8,128)(2,1)S(1)}, bf16[1408,512]{1,0:T(8,128)(2,1)S(1)}, u32[]{:S(2)}, u32[]{:S(2)}) %collective-permute-start.53) | collective-permute-done | bytes 1441824 | tf_op jit(solution)/shard_map/ppermute | solution.py:203
  570.8 28.5 %collective-permute-done.47.refs_6_ = bf16[1408,512]{1,0:T(8,128)(2,1)S(1)} collective-permute-done((bf16[1408,512]{1,0:T(8,128)(2,1)S(1)}, bf16[1408,512]{1,0:T(8,128)(2,1)S(1)}, u32[]{:S(2)}, u32[]{:S(2)}) %collective-permute-start.47) | collective-permute-done | bytes 1441824 | tf_op jit(solution)/shard_map/ppermute | solution.py:203
  601.5 28.6 %collective-permute-done.41.refs_6_ = bf16[1408,512]{1,0:T(8,128)(2,1)S(1)} collective-permute-done((bf16[1408,512]{1,0:T(8,128)(2,1)S(1)}, bf16[1408,512]{1,0:T(8,128)(2,1)S(1)}, u32[]{:S(2)}, u32[]{:S(2)}) %collective-permute-start.41) | collective-permute-done | bytes 1441824 | tf_op jit(solution)/shard_map/ppermute | solution.py:203
  632.2 28.8 %collective-permute-done.35.refs_6_ = bf16[1408,512]{1,0:T(8,128)(2,1)S(1)} collective-permute-done((bf16[1408,512]{1,0:T(8,128)(2,1)S(1)}, bf16[1408,512]{1,0:T(8,128)(2,1)S(1)}, u32[]{:S(2)}, u32[]{:S(2)}) %collective-permute-start.35) | collective-permute-done | bytes 1441824 | tf_op jit(solution)/shard_map/ppermute | solution.py:203
  663.1 28.8 %collective-permute-done.29.refs_6_ = bf16[1408,512]{1,0:T(8,128)(2,1)S(1)} collective-permute-done((bf16[1408,512]{1,0:T(8,128)(2,1)S(1)}, bf16[1408,512]{1,0:T(8,128)(2,1)S(1)}, u32[]{:S(2)}, u32[]{:S(2)}) %collective-permute-start.29) | collective-permute-done | bytes 1441824 | tf_op jit(solution)/shard_map/ppermute | solution.py:203
  694.9 28.0 %collective-permute-done.23.refs_6_ = bf16[1408,512]{1,0:T(8,128)(2,1)S(1)} collective-permute-done((bf16[1408,512]{1,0:T(8,128)(2,1)S(1)}, bf16[1408,512]{1,0:T(8,128)(2,1)S(1)}, u32[]{:S(2)}, u32[]{:S(2)}) %collective-permute-start.23) | collective-permute-done | bytes 1441824 | tf_op jit(solution)/shard_map/ppermute | solution.py:203
  725.6 5.2 shard_map.67.refs_7_
  730.9 5.2 shard_map.68.refs_7_
  736.1 5.2 shard_map.69.refs_7_
  741.4 5.2 shard_map.70.refs_7_
  746.6 5.2 shard_map.71.refs_7_
  751.8 5.2 shard_map.72.refs_7_
  757.1 5.2 shard_map.73.refs_7_
  762.3 14.0 %collective-permute-done.11.refs_6_ = bf16[1024,512]{1,0:T(8,128)(2,1)} collective-permute-done((bf16[1024,512]{1,0:T(8,128)(2,1)}, bf16[1024,512]{1,0:T(8,128)(2,1)}, u32[]{:S(2)}, u32[]{:S(2)}) %collective-permute-start.11) | collective-permute-done | bytes 1048608 | tf_op jit(solution)/shard_map/ppermute | solution.py:203
  776.3 4.2 shard_map.74.refs_7_
  782.8 3.7 shard_map.75
  (161 shorter events, 80.4 us)
Async XLA Ops:
  31.5 42.8 %collective-permute-start.6 = (bf16[1024,512]{1,0:T(8,128)(2,1)}, bf16[1024,512]{1,0:T(8,128)(2,1)}, u32[]{:S(2)}, u32[]{:S(2)}) collective-permute-start(bf16[1024,512]{1,0:T(8,128)(2,1)} %shard_map.60.refs_0_), channel_id=1, source_target_pairs={{0,1},{1,2},{2,3},{4,5},{5,6},{6,7},{8,9},{9,10},{10,11},{12,13},{... | collective-permute-start | bytes 3145736 | tf_op jit(solution)/shard_map/ppermute | solution.py:202
  48.3 68.4 %collective-permute-start.48 = (bf16[1408,512]{1,0:T(8,128)(2,1)S(1)}, bf16[1408,512]{1,0:T(8,128)(2,1)}, u32[]{:S(2)}, u32[]{:S(2)}) collective-permute-start(bf16[1408,512]{1,0:T(8,128)(2,1)S(1)} %get-tuple-element.7.refs_0_), channel_id=1, source_target_pairs={{0,1},{1,2},{2,3},{4,5},{5,6},{6,7},{8,9},{9,10},{10,11},{12,13},{... | collective-permute-start | bytes 4325384 | tf_op jit(solution)/shard_map/ppermute | solution.py:202
  54.1 67.1 %collective-permute-start.49 = (bf16[1408,512]{1,0:T(8,128)(2,1)S(1)}, bf16[1408,512]{1,0:T(8,128)(2,1)}, u32[]{:S(2)}, u32[]{:S(2)}) collective-permute-start(bf16[1408,512]{1,0:T(8,128)(2,1)S(1)} %get-tuple-element.7.refs_0_), channel_id=1, source_target_pairs={{1,0},{2,1},{3,2},{5,4},{6,5},{7,6},{9,8},{10,9},{11,10},{13,12},{... | collective-permute-start | bytes 4325384 | tf_op jit(solution)/shard_map/ppermute | solution.py:203
  58.6 68.3 %collective-permute-start.42 = (bf16[1408,512]{1,0:T(8,128)(2,1)}, bf16[1408,512]{1,0:T(8,128)(2,1)}, u32[]{:S(2)}, u32[]{:S(2)}) collective-permute-start(bf16[1408,512]{1,0:T(8,128)(2,1)} %shard_map.66.refs_0_), channel_id=1, source_target_pairs={{0,1},{1,2},{2,3},{4,5},{5,6},{6,7},{8,9},{9,10},{10,11},{12,13},{... | collective-permute-start | bytes 4325384 | tf_op jit(solution)/shard_map/ppermute | solution.py:202
  74.3 70.0 %collective-permute-start.43 = (bf16[1408,512]{1,0:T(8,128)(2,1)}, bf16[1408,512]{1,0:T(8,128)(2,1)}, u32[]{:S(2)}, u32[]{:S(2)}) collective-permute-start(bf16[1408,512]{1,0:T(8,128)(2,1)} %shard_map.66.refs_0_), channel_id=1, source_target_pairs={{1,0},{2,1},{3,2},{5,4},{6,5},{7,6},{9,8},{10,9},{11,10},{13,12},{... | collective-permute-start | bytes 4325384 | tf_op jit(solution)/shard_map/ppermute | solution.py:203
  116.7 58.5 %collective-permute-start.37 = (bf16[1408,512]{1,0:T(8,128)(2,1)}, bf16[1408,512]{1,0:T(8,128)(2,1)}, u32[]{:S(2)}, u32[]{:S(2)}) collective-permute-start(bf16[1408,512]{1,0:T(8,128)(2,1)} %shard_map.65.refs_0_), channel_id=1, source_target_pairs={{1,0},{2,1},{3,2},{5,4},{6,5},{7,6},{9,8},{10,9},{11,10},{13,12},{... | collective-permute-start | bytes 4325384 | tf_op jit(solution)/shard_map/ppermute | solution.py:203
  121.2 63.4 %collective-permute-start.30 = (bf16[1408,512]{1,0:T(8,128)(2,1)}, bf16[1408,512]{1,0:T(8,128)(2,1)}, u32[]{:S(2)}, u32[]{:S(2)}) collective-permute-start(bf16[1408,512]{1,0:T(8,128)(2,1)} %shard_map.64.refs_0_), channel_id=1, source_target_pairs={{0,1},{1,2},{2,3},{4,5},{5,6},{6,7},{8,9},{9,10},{10,11},{12,13},{... | collective-permute-start | bytes 4325384 | tf_op jit(solution)/shard_map/ppermute | solution.py:202
  126.9 79.2 %collective-permute-start.31 = (bf16[1408,512]{1,0:T(8,128)(2,1)}, bf16[1408,512]{1,0:T(8,128)(2,1)}, u32[]{:S(2)}, u32[]{:S(2)}) collective-permute-start(bf16[1408,512]{1,0:T(8,128)(2,1)} %shard_map.64.refs_0_), channel_id=1, source_target_pairs={{1,0},{2,1},{3,2},{5,4},{6,5},{7,6},{9,8},{10,9},{11,10},{13,12},{... | collective-permute-start | bytes 4325384 | tf_op jit(solution)/shard_map/ppermute | solution.py:203
  144.3 71.2 %collective-permute-start.24 = (bf16[1408,512]{1,0:T(8,128)(2,1)}, bf16[1408,512]{1,0:T(8,128)(2,1)}, u32[]{:S(2)}, u32[]{:S(2)}) collective-permute-start(bf16[1408,512]{1,0:T(8,128)(2,1)} %shard_map.63.refs_0_), channel_id=1, source_target_pairs={{0,1},{1,2},{2,3},{4,5},{5,6},{6,7},{8,9},{9,10},{10,11},{12,13},{... | collective-permute-start | bytes 4325384 | tf_op jit(solution)/shard_map/ppermute | solution.py:202
  153.7 83.3 %collective-permute-start.25 = (bf16[1408,512]{1,0:T(8,128)(2,1)S(1)}, bf16[1408,512]{1,0:T(8,128)(2,1)}, u32[]{:S(2)}, u32[]{:S(2)}) collective-permute-start(bf16[1408,512]{1,0:T(8,128)(2,1)S(1)} %copy-done.6), channel_id=1, source_target_pairs={{1,0},{2,1},{3,2},{5,4},{6,5},{7,6},{9,8},{10,9},{11,10},{13,12},{... | collective-permute-start | bytes 4325384 | tf_op jit(solution)/shard_map/ppermute | solution.py:203
  175.2 71.2 %collective-permute-start.18 = (bf16[1408,512]{1,0:T(8,128)(2,1)}, bf16[1408,512]{1,0:T(8,128)(2,1)}, u32[]{:S(2)}, u32[]{:S(2)}) collective-permute-start(bf16[1408,512]{1,0:T(8,128)(2,1)} %shard_map.62.refs_0_), channel_id=1, source_target_pairs={{0,1},{1,2},{2,3},{4,5},{5,6},{6,7},{8,9},{9,10},{10,11},{12,13},{... | collective-permute-start | bytes 4325384 | tf_op jit(solution)/shard_map/ppermute | solution.py:202
  184.6 83.2 %collective-permute-start.19 = (bf16[1408,512]{1,0:T(8,128)(2,1)S(1)}, bf16[1408,512]{1,0:T(8,128)(2,1)S(1)}, u32[]{:S(2)}, u32[]{:S(2)}) collective-permute-start(bf16[1408,512]{1,0:T(8,128)(2,1)S(1)} %copy-done.5), channel_id=1, source_target_pairs={{1,0},{2,1},{3,2},{5,4},{6,5},{7,6},{9,8},{10,9},{11,10},{13,12},{... | collective-permute-start | bytes 4325384 | tf_op jit(solution)/shard_map/ppermute | solution.py:203
  206.1 69.6 %collective-permute-start.12 = (bf16[1408,512]{1,0:T(8,128)(2,1)}, bf16[1408,512]{1,0:T(8,128)(2,1)S(1)}, u32[]{:S(2)}, u32[]{:S(2)}) collective-permute-start(bf16[1408,512]{1,0:T(8,128)(2,1)} %shard_map.61.refs_0_), channel_id=1, source_target_pairs={{0,1},{1,2},{2,3},{4,5},{5,6},{6,7},{8,9},{9,10},{10,11},{12,13},{... | collective-permute-start | bytes 4325384 | tf_op jit(solution)/shard_map/ppermute | solution.py:202
  215.5 83.2 %collective-permute-start.13 = (bf16[1408,512]{1,0:T(8,128)(2,1)}, bf16[1408,512]{1,0:T(8,128)(2,1)S(1)}, u32[]{:S(2)}, u32[]{:S(2)}) collective-permute-start(bf16[1408,512]{1,0:T(8,128)(2,1)} %shard_map.61.refs_0_), channel_id=1, source_target_pairs={{1,0},{2,1},{3,2},{5,4},{6,5},{7,6},{9,8},{10,9},{11,10},{13,12},{... | collective-permute-start | bytes 4325384 | tf_op jit(solution)/shard_map/ppermute | solution.py:203
  237.0 62.4 %collective-permute-start.8 = (bf16[1024,512]{1,0:T(8,128)(2,1)}, bf16[1024,512]{1,0:T(8,128)(2,1)}, u32[]{:S(2)}, u32[]{:S(2)}) collective-permute-start(bf16[1024,512]{1,0:T(8,128)(2,1)} %collective-permute-done.6.refs_1_), channel_id=1, source_target_pairs={{1,2},{2,3},{5,6},{6,7},{9,10},{10,11},{13,14},{14,15},{17,18},{18... | collective-permute-start | bytes 3145736 | tf_op jit(solution)/shard_map/ppermute | solution.py:202
  246.4 74.9 %collective-permute-start.9 = (bf16[1024,512]{1,0:T(8,128)(2,1)}, bf16[1024,512]{1,0:T(8,128)(2,1)}, u32[]{:S(2)}, u32[]{:S(2)}) collective-permute-start(bf16[1024,512]{1,0:T(8,128)(2,1)} %collective-permute-done.7.refs_2_), channel_id=1, source_target_pairs={{1,0},{2,1},{5,4},{6,5},{9,8},{10,9},{13,12},{14,13},{17,16},{18,1... | collective-permute-start | bytes 3145736 | tf_op jit(solution)/shard_map/ppermute | solution.py:203
  267.8 54.2 %collective-permute-start.50 = (bf16[1408,512]{1,0:T(8,128)(2,1)}, bf16[1408,512]{1,0:T(8,128)(2,1)S(1)}, u32[]{:S(2)}, u32[]{:S(2)}) collective-permute-start(bf16[1408,512]{1,0:T(8,128)(2,1)} %collective-permute-done.48.refs_1_), channel_id=1, source_target_pairs={{1,2},{2,3},{5,6},{6,7},{9,10},{10,11},{13,14},{14,15},{17,18},{18... | collective-permute-start | bytes 4325384 | tf_op jit(solution)/shard_map/ppermute | solution.py:202
  275.7 76.4 %collective-permute-start.51 = (bf16[1408,512]{1,0:T(8,128)(2,1)}, bf16[1408,512]{1,0:T(8,128)(2,1)S(1)}, u32[]{:S(2)}, u32[]{:S(2)}) collective-permute-start(bf16[1408,512]{1,0:T(8,128)(2,1)} %collective-permute-done.49.refs_2_), channel_id=1, source_target_pairs={{1,0},{2,1},{5,4},{6,5},{9,8},{10,9},{13,12},{14,13},{17,16},{18,1... | collective-permute-start | bytes 4325384 | tf_op jit(solution)/shard_map/ppermute | solution.py:203
  298.7 54.1 %collective-permute-start.44 = (bf16[1408,512]{1,0:T(8,128)(2,1)}, bf16[1408,512]{1,0:T(8,128)(2,1)S(1)}, u32[]{:S(2)}, u32[]{:S(2)}) collective-permute-start(bf16[1408,512]{1,0:T(8,128)(2,1)} %collective-permute-done.42.refs_1_), channel_id=1, source_target_pairs={{1,2},{2,3},{5,6},{6,7},{9,10},{10,11},{13,14},{14,15},{17,18},{18... | collective-permute-start | bytes 4325384 | tf_op jit(solution)/shard_map/ppermute | solution.py:202
  299.4 83.5 %collective-permute-start.45 = (bf16[1408,512]{1,0:T(8,128)(2,1)}, bf16[1408,512]{1,0:T(8,128)(2,1)S(1)}, u32[]{:S(2)}, u32[]{:S(2)}) collective-permute-start(bf16[1408,512]{1,0:T(8,128)(2,1)} %collective-permute-done.43.refs_2_), channel_id=1, source_target_pairs={{1,0},{2,1},{5,4},{6,5},{9,8},{10,9},{13,12},{14,13},{17,16},{18,1... | collective-permute-start | bytes 4325384 | tf_op jit(solution)/shard_map/ppermute | solution.py:203
  321.3 62.4 %collective-permute-start.38 = (bf16[1408,512]{1,0:T(8,128)(2,1)}, bf16[1408,512]{1,0:T(8,128)(2,1)S(1)}, u32[]{:S(2)}, u32[]{:S(2)}) collective-permute-start(bf16[1408,512]{1,0:T(8,128)(2,1)} %collective-permute-done.36.refs_1_), channel_id=1, source_target_pairs={{1,2},{2,3},{5,6},{6,7},{9,10},{10,11},{13,14},{14,15},{17,18},{18... | collective-permute-start | bytes 4325384 | tf_op jit(solution)/shard_map/ppermute | solution.py:202
  322.0 91.8 %collective-permute-start.39 = (bf16[1408,512]{1,0:T(8,128)(2,1)}, bf16[1408,512]{1,0:T(8,128)(2,1)S(1)}, u32[]{:S(2)}, u32[]{:S(2)}) collective-permute-start(bf16[1408,512]{1,0:T(8,128)(2,1)} %collective-permute-done.37.refs_2_), channel_id=1, source_target_pairs={{1,0},{2,1},{5,4},{6,5},{9,8},{10,9},{13,12},{14,13},{17,16},{18,1... | collective-permute-start | bytes 4325384 | tf_op jit(solution)/shard_map/ppermute | solution.py:203
  352.0 62.5 %collective-permute-start.32 = (bf16[1408,512]{1,0:T(8,128)(2,1)}, bf16[1408,512]{1,0:T(8,128)(2,1)S(1)}, u32[]{:S(2)}, u32[]{:S(2)}) collective-permute-start(bf16[1408,512]{1,0:T(8,128)(2,1)} %collective-permute-done.30.refs_1_), channel_id=1, source_target_pairs={{1,2},{2,3},{5,6},{6,7},{9,10},{10,11},{13,14},{14,15},{17,18},{18... | collective-permute-start | bytes 4325384 | tf_op jit(solution)/shard_map/ppermute | solution.py:202
  352.8 91.9 %collective-permute-start.33 = (bf16[1408,512]{1,0:T(8,128)(2,1)}, bf16[1408,512]{1,0:T(8,128)(2,1)S(1)}, u32[]{:S(2)}, u32[]{:S(2)}) collective-permute-start(bf16[1408,512]{1,0:T(8,128)(2,1)} %collective-permute-done.31.refs_2_), channel_id=1, source_target_pairs={{1,0},{2,1},{5,4},{6,5},{9,8},{10,9},{13,12},{14,13},{17,16},{18,1... | collective-permute-start | bytes 4325384 | tf_op jit(solution)/shard_map/ppermute | solution.py:203
  382.9 62.5 %collective-permute-start.26 = (bf16[1408,512]{1,0:T(8,128)(2,1)}, bf16[1408,512]{1,0:T(8,128)(2,1)S(1)}, u32[]{:S(2)}, u32[]{:S(2)}) collective-permute-start(bf16[1408,512]{1,0:T(8,128)(2,1)} %collective-permute-done.24.refs_1_), channel_id=1, source_target_pairs={{1,2},{2,3},{5,6},{6,7},{9,10},{10,11},{13,14},{14,15},{17,18},{18... | collective-permute-start | bytes 4325384 | tf_op jit(solution)/shard_map/ppermute | solution.py:202
  383.7 91.9 %collective-permute-start.27 = (bf16[1408,512]{1,0:T(8,128)(2,1)}, bf16[1408,512]{1,0:T(8,128)(2,1)S(1)}, u32[]{:S(2)}, u32[]{:S(2)}) collective-permute-start(bf16[1408,512]{1,0:T(8,128)(2,1)} %collective-permute-done.25.refs_2_), channel_id=1, source_target_pairs={{1,0},{2,1},{5,4},{6,5},{9,8},{10,9},{13,12},{14,13},{17,16},{18,1... | collective-permute-start | bytes 4325384 | tf_op jit(solution)/shard_map/ppermute | solution.py:203
  413.8 62.5 %collective-permute-start.20 = (bf16[1408,512]{1,0:T(8,128)(2,1)}, bf16[1408,512]{1,0:T(8,128)(2,1)S(1)}, u32[]{:S(2)}, u32[]{:S(2)}) collective-permute-start(bf16[1408,512]{1,0:T(8,128)(2,1)} %collective-permute-done.18.refs_1_), channel_id=1, source_target_pairs={{1,2},{2,3},{5,6},{6,7},{9,10},{10,11},{13,14},{14,15},{17,18},{18... | collective-permute-start | bytes 4325384 | tf_op jit(solution)/shard_map/ppermute | solution.py:202
  414.6 91.9 %collective-permute-start.21 = (bf16[1408,512]{1,0:T(8,128)(2,1)S(1)}, bf16[1408,512]{1,0:T(8,128)(2,1)S(1)}, u32[]{:S(2)}, u32[]{:S(2)}) collective-permute-start(bf16[1408,512]{1,0:T(8,128)(2,1)S(1)} %collective-permute-done.19.refs_2_), channel_id=1, source_target_pairs={{1,0},{2,1},{5,4},{6,5},{9,8},{10,9},{13,12},{14,13},{17,16},{18,1... | collective-permute-start | bytes 4325384 | tf_op jit(solution)/shard_map/ppermute | solution.py:203
  444.7 62.5 %collective-permute-start.14 = (bf16[1408,512]{1,0:T(8,128)(2,1)S(1)}, bf16[1408,512]{1,0:T(8,128)(2,1)S(1)}, u32[]{:S(2)}, u32[]{:S(2)}) collective-permute-start(bf16[1408,512]{1,0:T(8,128)(2,1)S(1)} %collective-permute-done.12.refs_1_), channel_id=1, source_target_pairs={{1,2},{2,3},{5,6},{6,7},{9,10},{10,11},{13,14},{14,15},{17,18},{18... | collective-permute-start | bytes 4325384 | tf_op jit(solution)/shard_map/ppermute | solution.py:202
  445.5 92.0 %collective-permute-start.15 = (bf16[1408,512]{1,0:T(8,128)(2,1)S(1)}, bf16[1408,512]{1,0:T(8,128)(2,1)}, u32[]{:S(2)}, u32[]{:S(2)}) collective-permute-start(bf16[1408,512]{1,0:T(8,128)(2,1)S(1)} %collective-permute-done.13.refs_2_), channel_id=1, source_target_pairs={{1,0},{2,1},{5,4},{6,5},{9,8},{10,9},{13,12},{14,13},{17,16},{18,1... | collective-permute-start | bytes 4325384 | tf_op jit(solution)/shard_map/ppermute | solution.py:203
  475.6 62.6 %collective-permute-start.52 = (bf16[1408,512]{1,0:T(8,128)(2,1)S(1)}, bf16[1408,512]{1,0:T(8,128)(2,1)S(1)}, u32[]{:S(2)}, u32[]{:S(2)}) collective-permute-start(bf16[1408,512]{1,0:T(8,128)(2,1)S(1)} %collective-permute-done.50.refs_3_), channel_id=1, source_target_pairs={{2,3},{6,7},{10,11},{14,15},{18,19},{22,23},{26,27},{30,31}} | collective-permute-start | bytes 4325384 | tf_op jit(solution)/shard_map/ppermute | solution.py:202
  476.4 91.9 %collective-permute-start.53 = (bf16[1408,512]{1,0:T(8,128)(2,1)S(1)}, bf16[1408,512]{1,0:T(8,128)(2,1)S(1)}, u32[]{:S(2)}, u32[]{:S(2)}) collective-permute-start(bf16[1408,512]{1,0:T(8,128)(2,1)S(1)} %collective-permute-done.51.refs_4_), channel_id=1, source_target_pairs={{1,0},{5,4},{9,8},{13,12},{17,16},{21,20},{25,24},{29,28}} | collective-permute-start | bytes 4325384 | tf_op jit(solution)/shard_map/ppermute | solution.py:203
  506.5 62.9 %collective-permute-start.46 = (bf16[1408,512]{1,0:T(8,128)(2,1)S(1)}, bf16[1408,512]{1,0:T(8,128)(2,1)S(1)}, u32[]{:S(2)}, u32[]{:S(2)}) collective-permute-start(bf16[1408,512]{1,0:T(8,128)(2,1)S(1)} %collective-permute-done.44.refs_3_), channel_id=1, source_target_pairs={{2,3},{6,7},{10,11},{14,15},{18,19},{22,23},{26,27},{30,31}} | collective-permute-start | bytes 4325384 | tf_op jit(solution)/shard_map/ppermute | solution.py:202
  507.3 91.9 %collective-permute-start.47 = (bf16[1408,512]{1,0:T(8,128)(2,1)S(1)}, bf16[1408,512]{1,0:T(8,128)(2,1)S(1)}, u32[]{:S(2)}, u32[]{:S(2)}) collective-permute-start(bf16[1408,512]{1,0:T(8,128)(2,1)S(1)} %collective-permute-done.45.refs_4_), channel_id=1, source_target_pairs={{1,0},{5,4},{9,8},{13,12},{17,16},{21,20},{25,24},{29,28}} | collective-permute-start | bytes 4325384 | tf_op jit(solution)/shard_map/ppermute | solution.py:203
  537.5 62.5 %collective-permute-start.40 = (bf16[1408,512]{1,0:T(8,128)(2,1)S(1)}, bf16[1408,512]{1,0:T(8,128)(2,1)S(1)}, u32[]{:S(2)}, u32[]{:S(2)}) collective-permute-start(bf16[1408,512]{1,0:T(8,128)(2,1)S(1)} %collective-permute-done.38.refs_3_), channel_id=1, source_target_pairs={{2,3},{6,7},{10,11},{14,15},{18,19},{22,23},{26,27},{30,31}} | collective-permute-start | bytes 4325384 | tf_op jit(solution)/shard_map/ppermute | solution.py:202
  538.3 91.8 %collective-permute-start.41 = (bf16[1408,512]{1,0:T(8,128)(2,1)S(1)}, bf16[1408,512]{1,0:T(8,128)(2,1)S(1)}, u32[]{:S(2)}, u32[]{:S(2)}) collective-permute-start(bf16[1408,512]{1,0:T(8,128)(2,1)S(1)} %collective-permute-done.39.refs_4_), channel_id=1, source_target_pairs={{1,0},{5,4},{9,8},{13,12},{17,16},{21,20},{25,24},{29,28}} | collective-permute-start | bytes 4325384 | tf_op jit(solution)/shard_map/ppermute | solution.py:203
  568.3 62.5 %collective-permute-start.34 = (bf16[1408,512]{1,0:T(8,128)(2,1)S(1)}, bf16[1408,512]{1,0:T(8,128)(2,1)S(1)}, u32[]{:S(2)}, u32[]{:S(2)}) collective-permute-start(bf16[1408,512]{1,0:T(8,128)(2,1)S(1)} %collective-permute-done.32.refs_3_), channel_id=1, source_target_pairs={{2,3},{6,7},{10,11},{14,15},{18,19},{22,23},{26,27},{30,31}} | collective-permute-start | bytes 4325384 | tf_op jit(solution)/shard_map/ppermute | solution.py:202
  569.5 91.6 %collective-permute-start.35 = (bf16[1408,512]{1,0:T(8,128)(2,1)S(1)}, bf16[1408,512]{1,0:T(8,128)(2,1)S(1)}, u32[]{:S(2)}, u32[]{:S(2)}) collective-permute-start(bf16[1408,512]{1,0:T(8,128)(2,1)S(1)} %collective-permute-done.33.refs_4_), channel_id=1, source_target_pairs={{1,0},{5,4},{9,8},{13,12},{17,16},{21,20},{25,24},{29,28}} | collective-permute-start | bytes 4325384 | tf_op jit(solution)/shard_map/ppermute | solution.py:203
  599.2 62.5 %collective-permute-start.28 = (bf16[1408,512]{1,0:T(8,128)(2,1)S(1)}, bf16[1408,512]{1,0:T(8,128)(2,1)S(1)}, u32[]{:S(2)}, u32[]{:S(2)}) collective-permute-start(bf16[1408,512]{1,0:T(8,128)(2,1)S(1)} %collective-permute-done.26.refs_3_), channel_id=1, source_target_pairs={{2,3},{6,7},{10,11},{14,15},{18,19},{22,23},{26,27},{30,31}} | collective-permute-start | bytes 4325384 | tf_op jit(solution)/shard_map/ppermute | solution.py:202
  600.0 91.9 %collective-permute-start.29 = (bf16[1408,512]{1,0:T(8,128)(2,1)S(1)}, bf16[1408,512]{1,0:T(8,128)(2,1)S(1)}, u32[]{:S(2)}, u32[]{:S(2)}) collective-permute-start(bf16[1408,512]{1,0:T(8,128)(2,1)S(1)} %collective-permute-done.27.refs_4_), channel_id=1, source_target_pairs={{1,0},{5,4},{9,8},{13,12},{17,16},{21,20},{25,24},{29,28}} | collective-permute-start | bytes 4325384 | tf_op jit(solution)/shard_map/ppermute | solution.py:203
  630.1 63.4 %collective-permute-start.22 = (bf16[1408,512]{1,0:T(8,128)(2,1)S(1)}, bf16[1408,512]{1,0:T(8,128)(2,1)S(1)}, u32[]{:S(2)}, u32[]{:S(2)}) collective-permute-start(bf16[1408,512]{1,0:T(8,128)(2,1)S(1)} %collective-permute-done.20.refs_3_), channel_id=1, source_target_pairs={{2,3},{6,7},{10,11},{14,15},{18,19},{22,23},{26,27},{30,31}} | collective-permute-start | bytes 4325384 | tf_op jit(solution)/shard_map/ppermute | solution.py:202
  630.9 91.9 %collective-permute-start.23 = (bf16[1408,512]{1,0:T(8,128)(2,1)S(1)}, bf16[1408,512]{1,0:T(8,128)(2,1)S(1)}, u32[]{:S(2)}, u32[]{:S(2)}) collective-permute-start(bf16[1408,512]{1,0:T(8,128)(2,1)S(1)} %collective-permute-done.21.refs_4_), channel_id=1, source_target_pairs={{1,0},{5,4},{9,8},{13,12},{17,16},{21,20},{25,24},{29,28}} | collective-permute-start | bytes 4325384 | tf_op jit(solution)/shard_map/ppermute | solution.py:203
  661.0 63.2 %collective-permute-start.16 = (bf16[1408,512]{1,0:T(8,128)(2,1)S(1)}, bf16[1408,512]{1,0:T(8,128)(2,1)S(1)}, u32[]{:S(2)}, u32[]{:S(2)}) collective-permute-start(bf16[1408,512]{1,0:T(8,128)(2,1)S(1)} %collective-permute-done.14.refs_3_), channel_id=1, source_target_pairs={{2,3},{6,7},{10,11},{14,15},{18,19},{22,23},{26,27},{30,31}} | collective-permute-start | bytes 4325384 | tf_op jit(solution)/shard_map/ppermute | solution.py:202
  661.8 95.3 %collective-permute-start.17 = (bf16[1408,512]{1,0:T(8,128)(2,1)}, bf16[1408,512]{1,0:T(8,128)(2,1)}, u32[]{:S(2)}, u32[]{:S(2)}) collective-permute-start(bf16[1408,512]{1,0:T(8,128)(2,1)} %collective-permute-done.15.refs_4_), channel_id=1, source_target_pairs={{1,0},{5,4},{9,8},{13,12},{17,16},{21,20},{25,24},{29,28}} | collective-permute-start | bytes 4325384 | tf_op jit(solution)/shard_map/ppermute | solution.py:203
  691.9 70.4 %collective-permute-start.10 = (bf16[1024,512]{1,0:T(8,128)(2,1)}, bf16[1024,512]{1,0:T(8,128)(2,1)}, u32[]{:S(2)}, u32[]{:S(2)}) collective-permute-start(bf16[1024,512]{1,0:T(8,128)(2,1)} %collective-permute-done.8.refs_3_), channel_id=1, source_target_pairs={{2,3},{6,7},{10,11},{14,15},{18,19},{22,23},{26,27},{30,31}} | collective-permute-start | bytes 3145736 | tf_op jit(solution)/shard_map/ppermute | solution.py:202
  693.6 82.7 %collective-permute-start.11 = (bf16[1024,512]{1,0:T(8,128)(2,1)}, bf16[1024,512]{1,0:T(8,128)(2,1)}, u32[]{:S(2)}, u32[]{:S(2)}) collective-permute-start(bf16[1024,512]{1,0:T(8,128)(2,1)} %collective-permute-done.9.refs_4_), channel_id=1, source_target_pairs={{1,0},{5,4},{9,8},{13,12},{17,16},{21,20},{25,24},{29,28}} | collective-permute-start | bytes 3145736 | tf_op jit(solution)/shard_map/ppermute | solution.py:203
  722.8 57.7 %collective-permute-start.4 = (bf16[384,512]{1,0:T(8,128)(2,1)}, bf16[384,512]{1,0:T(8,128)(2,1)}, u32[]{:S(2)}, u32[]{:S(2)}) collective-permute-start(bf16[384,512]{1,0:T(8,128)(2,1)} %collective-permute-done.2.refs_3_), channel_id=1, source_target_pairs={{2,3},{6,7},{10,11},{14,15},{18,19},{22,23},{26,27},{30,31}} | collective-permute-start | bytes 1179656 | tf_op jit(solution)/shard_map/ppermute | solution.py:202
  724.2 58.6 %collective-permute-start.5 = (bf16[384,512]{1,0:T(8,128)(2,1)}, bf16[384,512]{1,0:T(8,128)(2,1)}, u32[]{:S(2)}, u32[]{:S(2)}) collective-permute-start(bf16[384,512]{1,0:T(8,128)(2,1)} %collective-permute-done.3.refs_4_), channel_id=1, source_target_pairs={{1,0},{5,4},{9,8},{13,12},{17,16},{21,20},{25,24},{29,28}} | collective-permute-start | bytes 1179656 | tf_op jit(solution)/shard_map/ppermute | solution.py:203
  (46 other events, 5144.6 us)

commit v2 on v1

v2 whole, which is shorter than its diff:
```python
import functools

import jax
import jax.numpy as jnp
from jax import lax
from jax.experimental import pallas as pl
from jax.experimental.pallas import tpu as pltpu
from jax.sharding import PartitionSpec as P


LANES = 128
LEAD = 2
TAIL = 128


def tile_max(ref, e, r):
    block = jnp.abs(ref[e, pl.ds(r, LANES), :LANES])
    for c in range(LANES, ref.shape[2], LANES):
        block = jnp.maximum(block, jnp.abs(ref[e, pl.ds(r, LANES), c : c + LANES]))
    return jnp.max(block.T, axis=0, keepdims=True)


def normalise(values, scales):
    per_row = jnp.broadcast_to(scales, (LANES, LANES)).T
    parts = [values[:, c : c + LANES] / per_row for c in range(0, values.shape[1], LANES)]
    return jnp.concatenate(parts, axis=1).astype(jnp.bfloat16)


def to_all(ref, key, axis, here, size, sems):
    copies = [
        pltpu.make_async_remote_copy(
            src_ref=ref.at[key],
            dst_ref=ref.at[key],
            send_sem=sems.at[0, k],
            recv_sem=sems.at[1, k],
            device_id={axis: lax.rem(here + k, size)},
            device_id_type=pl.DeviceIdType.MESH,
        )
        for k in range(1, size)
    ]
    for copy in copies:
        copy.start()
    return copies


def wait(copies):
    for copy in copies:
        copy.wait()


def spread_kernel(owners, rows_ref, table_ref, load_sem, sems_all):
    mine = lax.axis_index("owner")
    load = pltpu.make_async_copy(rows_ref, table_ref.at[mine], load_sem)
    load.start()
    barrier = pltpu.get_barrier_semaphore()
    for k in range(1, owners):
        pl.semaphore_signal(barrier, inc=1, device_id={"owner": lax.rem(mine + k, owners)}, device_id_type=pl.DeviceIdType.MESH)
    pl.semaphore_wait(barrier, owners - 1)
    load.wait()
    wait(to_all(table_ref, mine, "owner", mine, owners, sems_all))


def spread(table, owners):
    return pl.pallas_call(
        functools.partial(spread_kernel, owners),
        out_shape=jax.ShapeDtypeStruct((owners,) + table.shape, jnp.float32),
        in_specs=[pl.BlockSpec(memory_space=pltpu.VMEM)],
        out_specs=pl.BlockSpec(memory_space=pltpu.VMEM),
        scratch_shapes=[pltpu.SemaphoreType.DMA, pltpu.SemaphoreType.DMA((2, owners))],
        compiler_params=pltpu.CompilerParams(collective_id=1, has_side_effects=True),
        cost_estimate=pl.CostEstimate(flops=table.size * 512, bytes_accessed=table.size * 64, transcendentals=0),
    )(table)


def head_kernel(sizes, early, w_hbm, weight_ref, gain_ref, scale_ref, own_ref, table_ref, held, peak, w_sem, sems_peak, sems_row):
    n = sizes
    lead, depth, _ = held.shape
    me = lax.axis_index("rows")
    mesh_ids = pl.DeviceIdType.MESH
    loads = [pltpu.make_async_copy(w_hbm.at[e], held.at[e], w_sem.at[e]) for e in range(lead)]
    for load in loads:
        load.start()

    barrier = pltpu.get_barrier_semaphore()
    for k in range(1, n):
        pl.semaphore_signal(barrier, inc=1, device_id={"rows": lax.rem(me + k, n)}, device_id_type=mesh_ids)
    table_ref[me] = weight_ref[...] * gain_ref[...]

    for e in range(lead):
        loads[e].wait()
        for r in range(0, depth, LANES):
            peak[me, e : e + 1, r : r + LANES] = tile_max(held, e, r)
    pl.semaphore_wait(barrier, n - 1)
    routes = to_all(table_ref, me, "rows", me, n, sems_row)
    tops = to_all(peak, me, "rows", me, n, sems_peak)
    wait(tops)
    scale = peak[0]
    for k in range(1, n):
        scale = jnp.maximum(scale, peak[k])
    scale_ref[...] = scale
    for r in range(0, early, LANES):
        own_ref[pl.ds(r, LANES), :] = normalise(held[0, pl.ds(r, LANES), :], scale_ref[0:1, r : r + LANES])
    wait(routes)


def head(w_down, router_weight, router_gain, n, lead, early):
    _, depth, columns = w_down.shape
    width, share = router_weight.shape
    vmem = pl.BlockSpec(memory_space=pltpu.VMEM)
    dma = pltpu.SemaphoreType.DMA
    return pl.pallas_call(
        functools.partial(head_kernel, n, early),
        out_shape=(
            jax.ShapeDtypeStruct((lead, depth), jnp.float32),
            jax.ShapeDtypeStruct((early, columns), jnp.bfloat16),
            jax.ShapeDtypeStruct((n, share, width), jnp.float32),
        ),
        in_specs=[pl.BlockSpec(memory_space=pl.ANY), vmem, vmem],
        out_specs=(vmem, vmem, vmem),
        scratch_shapes=[
            pltpu.VMEM((lead, depth, columns), jnp.float32),
            pltpu.VMEM((n, lead, depth), jnp.float32),
            dma((lead,)),
            dma((2, n)),
            dma((2, n)),
        ],
        compiler_params=pltpu.CompilerParams(collective_id=0, has_side_effects=True, vmem_limit_bytes=48 * 2**20),
    )(w_down, router_weight.T, router_gain[None, :])


def maxes_kernel(w_ref, peak_ref):
    for r in range(0, w_ref.shape[1], LANES):
        peak_ref[0, 0:1, r : r + LANES] = tile_max(w_ref, 0, r)


def maxes(w_down, lead):
    experts, depth, columns = w_down.shape
    return pl.pallas_call(
        maxes_kernel,
        out_shape=jax.ShapeDtypeStruct((experts - lead, 1, depth), jnp.float32),
        grid=(experts - lead,),
        in_specs=[pl.BlockSpec((1, depth, columns), lambda e: (e + lead, 0, 0))],
        out_specs=pl.BlockSpec((1, 1, depth), lambda e: (e, 0, 0)),
        cost_estimate=pl.CostEstimate(flops=w_down.size * 2, bytes_accessed=w_down.size * 4, transcendentals=0),
    )(w_down)


def small_kernel(*refs):
    *scale_refs, table_ref, scale_out, router_out, wide = refs
    row = 0
    for ref in scale_refs:
        for e in range(ref.shape[0]):
            scale_out[row : row + 1, :] = ref[e]
            row += 1
    owners, n, share, width = table_ref.shape
    for o in range(owners):
        for z in range(n):
            wide[o * share : (o + 1) * share, z * width : (z + 1) * width] = table_ref[o, z]
    router_out[...] = wide[...].astype(jnp.bfloat16)


def small(parts, table):
    owners, n, share, width = table.shape
    return pl.pallas_call(
        small_kernel,
        out_shape=(
            jax.ShapeDtypeStruct((sum(p.shape[0] for p in parts), parts[0].shape[2]), jnp.float32),
            jax.ShapeDtypeStruct((owners * share, n * width), jnp.bfloat16),
        ),
        scratch_shapes=[pltpu.VMEM((owners * share, n * width), jnp.float32)],
        cost_estimate=pl.CostEstimate(flops=table.size * 8, bytes_accessed=table.size * 6, transcendentals=0),
    )(*parts, table)


def norm_kernel(step_rows, w_ref, scale_ref, own_ref):
    for r in range(0, step_rows, LANES):
        own_ref[pl.ds(r, LANES), :] = normalise(w_ref[0, pl.ds(r, LANES), :], scale_ref[0, 0:1, r : r + LANES])


def norm(w_down, scales, e, row, rows, base):
    columns = w_down.shape[2]
    step_rows = LANES if row else rows
    at = row // step_rows
    return pl.pallas_call(
        functools.partial(norm_kernel, step_rows),
        out_shape=jax.ShapeDtypeStruct((rows, columns), jnp.bfloat16),
        grid=(rows // step_rows,),
        in_specs=[
            pl.BlockSpec((1, step_rows, columns), lambda r: (e, at + r, 0)),
            pl.BlockSpec((1, 1, step_rows), lambda r: (e - base, 0, at + r)),
        ],
        out_specs=pl.BlockSpec((step_rows, columns), lambda r: (r, 0)),
        cost_estimate=pl.CostEstimate(flops=rows * columns * 8, bytes_accessed=rows * columns * 6, transcendentals=0),
    )(w_down, scales)


def place_kernel(offsets, n, me_ref, *refs):
    out = refs[-1]
    for offset, block in zip(offsets, refs):
        slot = me_ref[0] + offset
        columns = block.shape[1]

        @pl.when((slot >= 0) & (slot < n))
        def _():
            out[0, :, pl.ds(pl.multiple_of(slot * columns, LANES), columns)] = block[...]


def place(me, blocks, serve, shape, e, row):
    rows, columns = blocks[0].shape
    n = shape[2] // columns
    step_rows = LANES if row else (rows // 2 if rows % 32 == 0 else rows)
    at = row // step_rows

    def spec(offset):
        def index(r, me_ref):
            slot = me_ref[0] + offset
            return jnp.where((slot >= 0) & (slot < n), r, 0), 0

        return pl.BlockSpec((step_rows, columns), index)

    first = serve is None
    return pl.pallas_call(
        functools.partial(place_kernel, tuple(blocks), n),
        out_shape=jax.ShapeDtypeStruct(shape, jnp.bfloat16),
        grid_spec=pltpu.PrefetchScalarGridSpec(
            num_scalar_prefetch=1,
            grid=(rows // step_rows,),
            in_specs=[spec(offset) for offset in blocks] + ([] if first else [pl.BlockSpec(memory_space=pl.ANY)]),
            out_specs=pl.BlockSpec((1, step_rows, shape[2]), lambda r, _: (e, at + r, 0)),
        ),
        input_output_aliases={} if first else {1 + len(blocks): 0},
        cost_estimate=pl.CostEstimate(flops=rows * columns * 64, bytes_accessed=rows * columns * 22, transcendentals=0),
    )(me, *blocks.values(), *([] if first else [serve]))


def plan(experts, depth):
    cut = depth - TAIL
    last = [(experts - 1, 0, cut), (experts - 1, cut, TAIL)]
    return [(e, 0, depth) for e in range(experts - 1)] + last


def on_device(owners, n, w_down, router_weight, router_gain):
    me = lax.axis_index("rows")
    me_array = me.astype(jnp.int32).reshape((1,))
    experts, depth, columns = w_down.shape
    shape = (experts, depth, n * columns)
    lead = min(LEAD, experts)
    scale_lead, first, table = head(w_down, router_weight, router_gain, n, lead, depth)
    scales = [scale_lead[:, None, :]]
    chunks = plan(experts, depth)
    held = []
    serve = None
    for at in range(len(chunks) + n - 1):
        if at < len(chunks):
            held.append({0: first if at == 0 else norm(w_down, scales[chunks[at][0] >= lead], *chunks[at], 0 if chunks[at][0] < lead else lead)})
        for step in range(1, n):
            c = at - step + 1
            if 0 <= c < len(chunks):
                held[c][-step] = lax.ppermute(held[c][1 - step], "rows", [(i, i + 1) for i in range(step - 1, n - 1)])
                held[c][step] = lax.ppermute(held[c][step - 1], "rows", [(i + 1, i) for i in range(0, n - step)])
        if at == 1 and experts > lead:
            tops = maxes(w_down, lead)
            scale = tops
            for k in range(1, n):
                scale = jnp.maximum(scale, lax.ppermute(tops, "rows", [(i, (i + k) % n) for i in range(n)]))
            scales.append(scale)
        c = at - n + 1
        if c >= 0:
            serve = place(me_array, held[c], serve, shape, *chunks[c][:2])
    table = spread(table, owners)
    scale_down, router = small(scales, table)
    return (serve, scale_down, router.T)


def solution(mesh):
    owners, n = mesh.shape["owner"], mesh.shape["rows"]
    placed = (P("owner", None, "rows"), P("rows", "owner"), P("rows"))
    return jax.shard_map(
        functools.partial(on_device, owners, n),
        mesh=mesh,
        in_specs=placed,
        out_specs=(P("owner", None, None), P("owner", None), P()),
        check_vma=False,
    )
```

time: 790 us -> 818 us (1.035)
  Pallas kernels: 88.8 us -> 117 us
  starting transfers between devices: 96.3 us -> 105 us
    pallas_call x1 -> x4, Pallas kernels: 19.3 us -> 49.2 us  [the longest x1 28.3 us: head(): pl.pallas_call(functools.partial(head_kernel, n, early), out_shape=(jax.S...]
  transfers between devices with their start and end apart: 54 -> 57, of which waited for: 30 -> 28; matrix products, arithmetic and copies ran while one was open for 0% -> 0% of each run, Pallas kernels for 8% -> 13%
where the time goes in v2:
time: 818 us; the launch traced here: 816 us
  waiting for transfers between devices  589 us (72%)
  Pallas kernels  117 us (14%)
  starting transfers between devices  105 us (13%)
    ppermute x27, waiting for transfers between devices, on_device(): lax.ppermute(held[c][step - 1], 'rows', [(i + 1, i) for i in range(0, n -...  565 us
    ppermute x27, starting transfers between devices, on_device(): lax.ppermute(held[c][1 - step], 'rows', [(i, i + 1) for i in range(step -...  62.8 us
    pallas_call x9, Pallas kernels, place(): pl.pallas_call(functools.partial(place_kernel, tuple(blocks), n), out_sha...  43.6 us
    ppermute x27, starting transfers between devices, on_device(): lax.ppermute(held[c][step - 1], 'rows', [(i + 1, i) for i in range(0, n -...  35.1 us
    pallas_call x1, Pallas kernels, head(): pl.pallas_call(functools.partial(head_kernel, n, early), out_shape=(jax.S...  28.3 us
    pallas_call x8, Pallas kernels, norm(): pl.pallas_call(functools.partial(norm_kernel, step_rows), out_shape=jax.S...  24.2 us
    ppermute x27, waiting for transfers between devices, on_device(): lax.ppermute(held[c][1 - step], 'rows', [(i, i + 1) for i in range(step -...  21.7 us
  transfers between devices with their start and end apart: 57, of which 28 were waited for; matrix products, arithmetic and copies ran while one was open for 0% of the time, Pallas kernels for 13%

profile of v2, /device:TPU:0, one launch (start us, length us, event | category | flops | bytes accessed | tf_op | source)
XLA Modules:
  0.0 815.7 jit_solution(6197621304834858774)
XLA Ops:
  0.6 8.2 %shard_map.58 = f32[6,1,1408]{2,1,0:T(1,128)} custom-call(f32[8,1408,512]{2,1,0:T(8,128)} %w_ref.17), custom_call_target="tpu_custom_call" | custom-call | flops 11534336 | bytes 23068672 | tf_op jit(solution)/shard_map/pallas_call | solution.py:138
  23.1 3.2 collective-permute-start.9
  26.4 28.3 %shard_map.66 = (f32[2,1408]{1,0:T(2,128)S(1)}, bf16[1408,512]{1,0:T(8,128)(2,1)S(1)}, f32[4,8,512]{2,1,0:T(8,128)S(1)}) custom-call(f32[8,1408,512]{2,1,0:T(8,128)} %w_ref.17, f32[8,512]{1,0:T(8,128)S(1)} %bitcast.4, f32[1,512]{1,0:T(1,128)S(1)} %bitcast.5), custom_call_target="tpu_custom_call" | custom-call | tf_op jit(solution)/shard_map/pallas_call | solution.py:111
  55.3 5.3 collective-permute-start.51
  63.6 4.5 collective-permute-start.3
  69.4 21.7 %collective-permute-done.3.refs_1_ = bf16[128,512]{1,0:T(8,128)(2,1)S(1)} collective-permute-done((bf16[128,512]{1,0:T(8,128)(2,1)}, bf16[128,512]{1,0:T(8,128)(2,1)S(1)}, u32[]{:S(2)}, u32[]{:S(2)}) %collective-permute-start.3) | collective-permute-done | bytes 131104 | tf_op jit(solution)/shard_map/ppermute | solution.py:259
  95.3 3.3 shard_map.67.refs_0_
  102.3 5.8 collective-permute-start.45
  109.4 3.2 shard_map.65.refs_0_
  112.6 5.6 collective-permute-start.39
  119.5 3.2 shard_map.64.refs_0_
  122.7 14.8 %collective-permute-done.52.refs_2_ = bf16[1408,512]{1,0:T(8,128)(2,1)} collective-permute-done((bf16[1408,512]{1,0:T(8,128)(2,1)S(1)}, bf16[1408,512]{1,0:T(8,128)(2,1)}, u32[]{:S(2)}, u32[]{:S(2)}) %collective-permute-start.52) | collective-permute-done | bytes 1441824 | tf_op jit(solution)/shard_map/ppermute | solution.py:260
  137.6 5.7 collective-permute-start.33
  147.8 20.7 %collective-permute-done.46.refs_2_ = bf16[1408,512]{1,0:T(8,128)(2,1)} collective-permute-done((bf16[1408,512]{1,0:T(8,128)(2,1)}, bf16[1408,512]{1,0:T(8,128)(2,1)}, u32[]{:S(2)}, u32[]{:S(2)}) %collective-permute-start.46) | collective-permute-done | bytes 1441824 | tf_op jit(solution)/shard_map/ppermute | solution.py:260
  168.5 5.7 collective-permute-start.27
  174.2 3.2 shard_map.62.refs_0_
  178.9 20.5 %collective-permute-done.40.refs_2_ = bf16[1408,512]{1,0:T(8,128)(2,1)} collective-permute-done((bf16[1408,512]{1,0:T(8,128)(2,1)}, bf16[1408,512]{1,0:T(8,128)(2,1)}, u32[]{:S(2)}, u32[]{:S(2)}) %collective-permute-start.40) | collective-permute-done | bytes 1441824 | tf_op jit(solution)/shard_map/ppermute | solution.py:260
  199.4 5.7 collective-permute-start.21
  205.1 3.2 shard_map.61.refs_0_
  209.6 20.7 %collective-permute-done.34.refs_2_ = bf16[1408,512]{1,0:T(8,128)(2,1)} collective-permute-done((bf16[1408,512]{1,0:T(8,128)(2,1)}, bf16[1408,512]{1,0:T(8,128)(2,1)}, u32[]{:S(2)}, u32[]{:S(2)}) %collective-permute-start.34) | collective-permute-done | bytes 1441824 | tf_op jit(solution)/shard_map/ppermute | solution.py:260
  230.3 4.7 collective-permute-start.15
  236.2 24.9 %collective-permute-done.28.refs_2_ = bf16[1408,512]{1,0:T(8,128)(2,1)} collective-permute-done((bf16[1408,512]{1,0:T(8,128)(2,1)S(1)}, bf16[1408,512]{1,0:T(8,128)(2,1)}, u32[]{:S(2)}, u32[]{:S(2)}) %collective-permute-start.28) | collective-permute-done | bytes 1441824 | tf_op jit(solution)/shard_map/ppermute | solution.py:260
  264.2 27.8 %collective-permute-done.22.refs_2_ = bf16[1408,512]{1,0:T(8,128)(2,1)S(1)} collective-permute-done((bf16[1408,512]{1,0:T(8,128)(2,1)S(1)}, bf16[1408,512]{1,0:T(8,128)(2,1)S(1)}, u32[]{:S(2)}, u32[]{:S(2)}) %collective-permute-start.22) | collective-permute-done | bytes 1441824 | tf_op jit(solution)/shard_map/ppermute | solution.py:260
  294.0 28.8 %collective-permute-done.16.refs_2_ = bf16[1408,512]{1,0:T(8,128)(2,1)S(1)} collective-permute-done((bf16[1408,512]{1,0:T(8,128)(2,1)}, bf16[1408,512]{1,0:T(8,128)(2,1)S(1)}, u32[]{:S(2)}, u32[]{:S(2)}) %collective-permute-start.16) | collective-permute-done | bytes 1441824 | tf_op jit(solution)/shard_map/ppermute | solution.py:260
  324.9 26.1 %collective-permute-done.12.refs_4_ = bf16[1280,512]{1,0:T(8,128)(2,1)} collective-permute-done((bf16[1280,512]{1,0:T(8,128)(2,1)}, bf16[1280,512]{1,0:T(8,128)(2,1)}, u32[]{:S(2)}, u32[]{:S(2)}) %collective-permute-start.12) | collective-permute-done | bytes 1310752 | tf_op jit(solution)/shard_map/ppermute | solution.py:260
  353.1 28.7 %collective-permute-done.54.refs_4_ = bf16[1408,512]{1,0:T(8,128)(2,1)S(1)} collective-permute-done((bf16[1408,512]{1,0:T(8,128)(2,1)}, bf16[1408,512]{1,0:T(8,128)(2,1)S(1)}, u32[]{:S(2)}, u32[]{:S(2)}) %collective-permute-start.54) | collective-permute-done | bytes 1441824 | tf_op jit(solution)/shard_map/ppermute | solution.py:260
  383.9 28.8 %collective-permute-done.48.refs_4_ = bf16[1408,512]{1,0:T(8,128)(2,1)S(1)} collective-permute-done((bf16[1408,512]{1,0:T(8,128)(2,1)}, bf16[1408,512]{1,0:T(8,128)(2,1)S(1)}, u32[]{:S(2)}, u32[]{:S(2)}) %collective-permute-start.48) | collective-permute-done | bytes 1441824 | tf_op jit(solution)/shard_map/ppermute | solution.py:260
  414.8 28.8 %collective-permute-done.42.refs_4_ = bf16[1408,512]{1,0:T(8,128)(2,1)S(1)} collective-permute-done((bf16[1408,512]{1,0:T(8,128)(2,1)}, bf16[1408,512]{1,0:T(8,128)(2,1)S(1)}, u32[]{:S(2)}, u32[]{:S(2)}) %collective-permute-start.42) | collective-permute-done | bytes 1441824 | tf_op jit(solution)/shard_map/ppermute | solution.py:260
  445.7 28.8 %collective-permute-done.36.refs_4_ = bf16[1408,512]{1,0:T(8,128)(2,1)S(1)} collective-permute-done((bf16[1408,512]{1,0:T(8,128)(2,1)}, bf16[1408,512]{1,0:T(8,128)(2,1)S(1)}, u32[]{:S(2)}, u32[]{:S(2)}) %collective-permute-start.36) | collective-permute-done | bytes 1441824 | tf_op jit(solution)/shard_map/ppermute | solution.py:260
  476.6 28.8 %collective-permute-done.30.refs_4_ = bf16[1408,512]{1,0:T(8,128)(2,1)S(1)} collective-permute-done((bf16[1408,512]{1,0:T(8,128)(2,1)}, bf16[1408,512]{1,0:T(8,128)(2,1)S(1)}, u32[]{:S(2)}, u32[]{:S(2)}) %collective-permute-start.30) | collective-permute-done | bytes 1441824 | tf_op jit(solution)/shard_map/ppermute | solution.py:260
  507.5 28.8 %collective-permute-done.24.refs_4_ = bf16[1408,512]{1,0:T(8,128)(2,1)S(1)} collective-permute-done((bf16[1408,512]{1,0:T(8,128)(2,1)S(1)}, bf16[1408,512]{1,0:T(8,128)(2,1)S(1)}, u32[]{:S(2)}, u32[]{:S(2)}) %collective-permute-start.24) | collective-permute-done | bytes 1441824 | tf_op jit(solution)/shard_map/ppermute | solution.py:260
  538.4 28.9 %collective-permute-done.18.refs_4_ = bf16[1408,512]{1,0:T(8,128)(2,1)} collective-permute-done((bf16[1408,512]{1,0:T(8,128)(2,1)S(1)}, bf16[1408,512]{1,0:T(8,128)(2,1)}, u32[]{:S(2)}, u32[]{:S(2)}) %collective-permute-start.18) | collective-permute-done | bytes 1441824 | tf_op jit(solution)/shard_map/ppermute | solution.py:260
  569.4 28.7 %collective-permute-done.56.refs_6_ = bf16[1408,512]{1,0:T(8,128)(2,1)S(1)} collective-permute-done((bf16[1408,512]{1,0:T(8,128)(2,1)S(1)}, bf16[1408,512]{1,0:T(8,128)(2,1)S(1)}, u32[]{:S(2)}, u32[]{:S(2)}) %collective-permute-start.56) | collective-permute-done | bytes 1441824 | tf_op jit(solution)/shard_map/ppermute | solution.py:260
  600.6 28.4 %collective-permute-done.50.refs_6_ = bf16[1408,512]{1,0:T(8,128)(2,1)S(1)} collective-permute-done((bf16[1408,512]{1,0:T(8,128)(2,1)S(1)}, bf16[1408,512]{1,0:T(8,128)(2,1)S(1)}, u32[]{:S(2)}, u32[]{:S(2)}) %collective-permute-start.50) | collective-permute-done | bytes 1441824 | tf_op jit(solution)/shard_map/ppermute | solution.py:260
  631.1 28.8 %collective-permute-done.44.refs_6_ = bf16[1408,512]{1,0:T(8,128)(2,1)S(1)} collective-permute-done((bf16[1408,512]{1,0:T(8,128)(2,1)S(1)}, bf16[1408,512]{1,0:T(8,128)(2,1)S(1)}, u32[]{:S(2)}, u32[]{:S(2)}) %collective-permute-start.44) | collective-permute-done | bytes 1441824 | tf_op jit(solution)/shard_map/ppermute | solution.py:260
  662.0 28.8 %collective-permute-done.38.refs_6_ = bf16[1408,512]{1,0:T(8,128)(2,1)S(1)} collective-permute-done((bf16[1408,512]{1,0:T(8,128)(2,1)S(1)}, bf16[1408,512]{1,0:T(8,128)(2,1)S(1)}, u32[]{:S(2)}, u32[]{:S(2)}) %collective-permute-start.38) | collective-permute-done | bytes 1441824 | tf_op jit(solution)/shard_map/ppermute | solution.py:260
  692.9 28.8 %collective-permute-done.32.refs_6_ = bf16[1408,512]{1,0:T(8,128)(2,1)S(1)} collective-permute-done((bf16[1408,512]{1,0:T(8,128)(2,1)S(1)}, bf16[1408,512]{1,0:T(8,128)(2,1)S(1)}, u32[]{:S(2)}, u32[]{:S(2)}) %collective-permute-start.32) | collective-permute-done | bytes 1441824 | tf_op jit(solution)/shard_map/ppermute | solution.py:260
  725.0 27.6 %collective-permute-done.26.refs_6_ = bf16[1408,512]{1,0:T(8,128)(2,1)S(1)} collective-permute-done((bf16[1408,512]{1,0:T(8,128)(2,1)S(1)}, bf16[1408,512]{1,0:T(8,128)(2,1)S(1)}, u32[]{:S(2)}, u32[]{:S(2)}) %collective-permute-start.26) | collective-permute-done | bytes 1441824 | tf_op jit(solution)/shard_map/ppermute | solution.py:260
  755.3 10.9 %shard_map.77.refs_2_ = f32[8,4,8,512]{3,2,1,0:T(8,128)} custom-call(f32[4,8,512]{2,1,0:T(8,128)} %copy-done.1), custom_call_target="tpu_custom_call" | custom-call | flops 8388608 | bytes 1048576 | tf_op jit(solution)/shard_map/pallas_call | solution.py:64
  768.0 5.2 shard_map.68.refs_7_
  773.3 5.2 shard_map.69.refs_7_
  778.5 5.2 shard_map.70.refs_7_
  783.7 5.2 shard_map.71.refs_7_
  789.0 5.2 shard_map.72.refs_7_
  794.2 5.2 shard_map.73.refs_7_
  799.4 5.2 shard_map.74.refs_7_
  804.7 4.0 collective-permute-done.14.refs_6_
  808.7 4.9 shard_map.75.refs_7_
  (165 shorter events, 80.0 us)
Async XLA Ops:
  23.1 84.9 %collective-permute-start.9 = (bf16[1280,512]{1,0:T(8,128)(2,1)}, bf16[1280,512]{1,0:T(8,128)(2,1)}, u32[]{:S(2)}, u32[]{:S(2)}) collective-permute-start(bf16[1280,512]{1,0:T(8,128)(2,1)} %shard_map.60.refs_0_), channel_id=1, source_target_pairs={{0,1},{1,2},{2,3},{4,5},{5,6},{6,7},{8,9},{9,10},{10,11},{12,13},{... | collective-permute-start | bytes 3932168 | tf_op jit(solution)/shard_map/ppermute | solution.py:259
  55.3 63.0 %collective-permute-start.51 = (bf16[1408,512]{1,0:T(8,128)(2,1)S(1)}, bf16[1408,512]{1,0:T(8,128)(2,1)}, u32[]{:S(2)}, u32[]{:S(2)}) collective-permute-start(bf16[1408,512]{1,0:T(8,128)(2,1)S(1)} %get-tuple-element.9.refs_0_), channel_id=1, source_target_pairs={{0,1},{1,2},{2,3},{4,5},{5,6},{6,7},{8,9},{9,10},{10,11},{12,13},{... | collective-permute-start | bytes 4325384 | tf_op jit(solution)/shard_map/ppermute | solution.py:259
  60.5 52.1 %collective-permute-start.10 = (bf16[1280,512]{1,0:T(8,128)(2,1)S(1)}, bf16[1280,512]{1,0:T(8,128)(2,1)}, u32[]{:S(2)}, u32[]{:S(2)}) collective-permute-start(bf16[1280,512]{1,0:T(8,128)(2,1)S(1)} %copy-done.6), channel_id=1, source_target_pairs={{1,0},{2,1},{3,2},{5,4},{6,5},{7,6},{9,8},{10,9},{11,10},{13,12},{... | collective-permute-start | bytes 3932168 | tf_op jit(solution)/shard_map/ppermute | solution.py:260
  108.1 60.4 %collective-permute-start.46 = (bf16[1408,512]{1,0:T(8,128)(2,1)}, bf16[1408,512]{1,0:T(8,128)(2,1)}, u32[]{:S(2)}, u32[]{:S(2)}) collective-permute-start(bf16[1408,512]{1,0:T(8,128)(2,1)} %shard_map.67.refs_0_), channel_id=1, source_target_pairs={{1,0},{2,1},{3,2},{5,4},{6,5},{7,6},{9,8},{10,9},{11,10},{13,12},{... | collective-permute-start | bytes 4325384 | tf_op jit(solution)/shard_map/ppermute | solution.py:260
  112.6 64.8 %collective-permute-start.39 = (bf16[1408,512]{1,0:T(8,128)(2,1)}, bf16[1408,512]{1,0:T(8,128)(2,1)}, u32[]{:S(2)}, u32[]{:S(2)}) collective-permute-start(bf16[1408,512]{1,0:T(8,128)(2,1)} %shard_map.65.refs_0_), channel_id=1, source_target_pairs={{0,1},{1,2},{2,3},{4,5},{5,6},{6,7},{8,9},{9,10},{10,11},{12,13},{... | collective-permute-start | bytes 4325384 | tf_op jit(solution)/shard_map/ppermute | solution.py:259
  118.2 81.1 %collective-permute-start.40 = (bf16[1408,512]{1,0:T(8,128)(2,1)}, bf16[1408,512]{1,0:T(8,128)(2,1)}, u32[]{:S(2)}, u32[]{:S(2)}) collective-permute-start(bf16[1408,512]{1,0:T(8,128)(2,1)} %shard_map.65.refs_0_), channel_id=1, source_target_pairs={{1,0},{2,1},{3,2},{5,4},{6,5},{7,6},{9,8},{10,9},{11,10},{13,12},{... | collective-permute-start | bytes 4325384 | tf_op jit(solution)/shard_map/ppermute | solution.py:260
  137.6 70.7 %collective-permute-start.33 = (bf16[1408,512]{1,0:T(8,128)(2,1)}, bf16[1408,512]{1,0:T(8,128)(2,1)}, u32[]{:S(2)}, u32[]{:S(2)}) collective-permute-start(bf16[1408,512]{1,0:T(8,128)(2,1)} %shard_map.64.refs_0_), channel_id=1, source_target_pairs={{0,1},{1,2},{2,3},{4,5},{5,6},{6,7},{8,9},{9,10},{10,11},{12,13},{... | collective-permute-start | bytes 4325384 | tf_op jit(solution)/shard_map/ppermute | solution.py:259
  143.3 87.0 %collective-permute-start.34 = (bf16[1408,512]{1,0:T(8,128)(2,1)}, bf16[1408,512]{1,0:T(8,128)(2,1)}, u32[]{:S(2)}, u32[]{:S(2)}) collective-permute-start(bf16[1408,512]{1,0:T(8,128)(2,1)} %shard_map.64.refs_0_), channel_id=1, source_target_pairs={{1,0},{2,1},{3,2},{5,4},{6,5},{7,6},{9,8},{10,9},{11,10},{13,12},{... | collective-permute-start | bytes 4325384 | tf_op jit(solution)/shard_map/ppermute | solution.py:260
  168.5 66.5 %collective-permute-start.27 = (bf16[1408,512]{1,0:T(8,128)(2,1)}, bf16[1408,512]{1,0:T(8,128)(2,1)}, u32[]{:S(2)}, u32[]{:S(2)}) collective-permute-start(bf16[1408,512]{1,0:T(8,128)(2,1)} %shard_map.63.refs_0_), channel_id=1, source_target_pairs={{0,1},{1,2},{2,3},{4,5},{5,6},{6,7},{8,9},{9,10},{10,11},{12,13},{... | collective-permute-start | bytes 4325384 | tf_op jit(solution)/shard_map/ppermute | solution.py:259
  177.4 83.7 %collective-permute-start.28 = (bf16[1408,512]{1,0:T(8,128)(2,1)S(1)}, bf16[1408,512]{1,0:T(8,128)(2,1)}, u32[]{:S(2)}, u32[]{:S(2)}) collective-permute-start(bf16[1408,512]{1,0:T(8,128)(2,1)S(1)} %copy-done.5), channel_id=1, source_target_pairs={{1,0},{2,1},{3,2},{5,4},{6,5},{7,6},{9,8},{10,9},{11,10},{13,12},{... | collective-permute-start | bytes 4325384 | tf_op jit(solution)/shard_map/ppermute | solution.py:260
  199.4 63.5 %collective-permute-start.21 = (bf16[1408,512]{1,0:T(8,128)(2,1)}, bf16[1408,512]{1,0:T(8,128)(2,1)}, u32[]{:S(2)}, u32[]{:S(2)}) collective-permute-start(bf16[1408,512]{1,0:T(8,128)(2,1)} %shard_map.62.refs_0_), channel_id=1, source_target_pairs={{0,1},{1,2},{2,3},{4,5},{5,6},{6,7},{8,9},{9,10},{10,11},{12,13},{... | collective-permute-start | bytes 4325384 | tf_op jit(solution)/shard_map/ppermute | solution.py:259
  208.3 83.6 %collective-permute-start.22 = (bf16[1408,512]{1,0:T(8,128)(2,1)S(1)}, bf16[1408,512]{1,0:T(8,128)(2,1)S(1)}, u32[]{:S(2)}, u32[]{:S(2)}) collective-permute-start(bf16[1408,512]{1,0:T(8,128)(2,1)S(1)} %copy-done.4), channel_id=1, source_target_pairs={{1,0},{2,1},{3,2},{5,4},{6,5},{7,6},{9,8},{10,9},{11,10},{13,12},{... | collective-permute-start | bytes 4325384 | tf_op jit(solution)/shard_map/ppermute | solution.py:260
  230.3 62.4 %collective-permute-start.15 = (bf16[1408,512]{1,0:T(8,128)(2,1)}, bf16[1408,512]{1,0:T(8,128)(2,1)S(1)}, u32[]{:S(2)}, u32[]{:S(2)}) collective-permute-start(bf16[1408,512]{1,0:T(8,128)(2,1)} %shard_map.61.refs_0_), channel_id=1, source_target_pairs={{0,1},{1,2},{2,3},{4,5},{5,6},{6,7},{8,9},{9,10},{10,11},{12,13},{... | collective-permute-start | bytes 4325384 | tf_op jit(solution)/shard_map/ppermute | solution.py:259
  234.9 87.9 %collective-permute-start.16 = (bf16[1408,512]{1,0:T(8,128)(2,1)}, bf16[1408,512]{1,0:T(8,128)(2,1)S(1)}, u32[]{:S(2)}, u32[]{:S(2)}) collective-permute-start(bf16[1408,512]{1,0:T(8,128)(2,1)} %shard_map.61.refs_0_), channel_id=1, source_target_pairs={{1,0},{2,1},{3,2},{5,4},{6,5},{7,6},{9,8},{10,9},{11,10},{13,12},{... | collective-permute-start | bytes 4325384 | tf_op jit(solution)/shard_map/ppermute | solution.py:260
  261.2 62.4 %collective-permute-start.11 = (bf16[1280,512]{1,0:T(8,128)(2,1)}, bf16[1280,512]{1,0:T(8,128)(2,1)}, u32[]{:S(2)}, u32[]{:S(2)}) collective-permute-start(bf16[1280,512]{1,0:T(8,128)(2,1)} %collective-permute-done.9.refs_1_), channel_id=1, source_target_pairs={{1,2},{2,3},{5,6},{6,7},{9,10},{10,11},{13,14},{14,15},{17,18},{18... | collective-permute-start | bytes 3932168 | tf_op jit(solution)/shard_map/ppermute | solution.py:259
  262.9 88.2 %collective-permute-start.12 = (bf16[1280,512]{1,0:T(8,128)(2,1)}, bf16[1280,512]{1,0:T(8,128)(2,1)}, u32[]{:S(2)}, u32[]{:S(2)}) collective-permute-start(bf16[1280,512]{1,0:T(8,128)(2,1)} %collective-permute-done.10.refs_2_), channel_id=1, source_target_pairs={{1,0},{2,1},{5,4},{6,5},{9,8},{10,9},{13,12},{14,13},{17,16},{18,1... | collective-permute-start | bytes 3932168 | tf_op jit(solution)/shard_map/ppermute | solution.py:260
  292.0 59.8 %collective-permute-start.53 = (bf16[1408,512]{1,0:T(8,128)(2,1)}, bf16[1408,512]{1,0:T(8,128)(2,1)S(1)}, u32[]{:S(2)}, u32[]{:S(2)}) collective-permute-start(bf16[1408,512]{1,0:T(8,128)(2,1)} %collective-permute-done.51.refs_1_), channel_id=1, source_target_pairs={{1,2},{2,3},{5,6},{6,7},{9,10},{10,11},{13,14},{14,15},{17,18},{18... | collective-permute-start | bytes 4325384 | tf_op jit(solution)/shard_map/ppermute | solution.py:259
  292.7 89.1 %collective-permute-start.54 = (bf16[1408,512]{1,0:T(8,128)(2,1)}, bf16[1408,512]{1,0:T(8,128)(2,1)S(1)}, u32[]{:S(2)}, u32[]{:S(2)}) collective-permute-start(bf16[1408,512]{1,0:T(8,128)(2,1)} %collective-permute-done.52.refs_2_), channel_id=1, source_target_pairs={{1,0},{2,1},{5,4},{6,5},{9,8},{10,9},{13,12},{14,13},{17,16},{18,1... | collective-permute-start | bytes 4325384 | tf_op jit(solution)/shard_map/ppermute | solution.py:260
  322.8 59.7 %collective-permute-start.47 = (bf16[1408,512]{1,0:T(8,128)(2,1)}, bf16[1408,512]{1,0:T(8,128)(2,1)S(1)}, u32[]{:S(2)}, u32[]{:S(2)}) collective-permute-start(bf16[1408,512]{1,0:T(8,128)(2,1)} %collective-permute-done.45.refs_1_), channel_id=1, source_target_pairs={{1,2},{2,3},{5,6},{6,7},{9,10},{10,11},{13,14},{14,15},{17,18},{18... | collective-permute-start | bytes 4325384 | tf_op jit(solution)/shard_map/ppermute | solution.py:259
  323.6 89.1 %collective-permute-start.48 = (bf16[1408,512]{1,0:T(8,128)(2,1)}, bf16[1408,512]{1,0:T(8,128)(2,1)S(1)}, u32[]{:S(2)}, u32[]{:S(2)}) collective-permute-start(bf16[1408,512]{1,0:T(8,128)(2,1)} %collective-permute-done.46.refs_2_), channel_id=1, source_target_pairs={{1,0},{2,1},{5,4},{6,5},{9,8},{10,9},{13,12},{14,13},{17,16},{18,1... | collective-permute-start | bytes 4325384 | tf_op jit(solution)/shard_map/ppermute | solution.py:260
  351.0 62.4 %collective-permute-start.41 = (bf16[1408,512]{1,0:T(8,128)(2,1)}, bf16[1408,512]{1,0:T(8,128)(2,1)S(1)}, u32[]{:S(2)}, u32[]{:S(2)}) collective-permute-start(bf16[1408,512]{1,0:T(8,128)(2,1)} %collective-permute-done.39.refs_1_), channel_id=1, source_target_pairs={{1,2},{2,3},{5,6},{6,7},{9,10},{10,11},{13,14},{14,15},{17,18},{18... | collective-permute-start | bytes 4325384 | tf_op jit(solution)/shard_map/ppermute | solution.py:259
  351.8 91.8 %collective-permute-start.42 = (bf16[1408,512]{1,0:T(8,128)(2,1)}, bf16[1408,512]{1,0:T(8,128)(2,1)S(1)}, u32[]{:S(2)}, u32[]{:S(2)}) collective-permute-start(bf16[1408,512]{1,0:T(8,128)(2,1)} %collective-permute-done.40.refs_2_), channel_id=1, source_target_pairs={{1,0},{2,1},{5,4},{6,5},{9,8},{10,9},{13,12},{14,13},{17,16},{18,1... | collective-permute-start | bytes 4325384 | tf_op jit(solution)/shard_map/ppermute | solution.py:260
  381.8 62.5 %collective-permute-start.35 = (bf16[1408,512]{1,0:T(8,128)(2,1)}, bf16[1408,512]{1,0:T(8,128)(2,1)S(1)}, u32[]{:S(2)}, u32[]{:S(2)}) collective-permute-start(bf16[1408,512]{1,0:T(8,128)(2,1)} %collective-permute-done.33.refs_1_), channel_id=1, source_target_pairs={{1,2},{2,3},{5,6},{6,7},{9,10},{10,11},{13,14},{14,15},{17,18},{18... | collective-permute-start | bytes 4325384 | tf_op jit(solution)/shard_map/ppermute | solution.py:259
  382.6 91.9 %collective-permute-start.36 = (bf16[1408,512]{1,0:T(8,128)(2,1)}, bf16[1408,512]{1,0:T(8,128)(2,1)S(1)}, u32[]{:S(2)}, u32[]{:S(2)}) collective-permute-start(bf16[1408,512]{1,0:T(8,128)(2,1)} %collective-permute-done.34.refs_2_), channel_id=1, source_target_pairs={{1,0},{2,1},{5,4},{6,5},{9,8},{10,9},{13,12},{14,13},{17,16},{18,1... | collective-permute-start | bytes 4325384 | tf_op jit(solution)/shard_map/ppermute | solution.py:260
  412.7 62.5 %collective-permute-start.29 = (bf16[1408,512]{1,0:T(8,128)(2,1)}, bf16[1408,512]{1,0:T(8,128)(2,1)S(1)}, u32[]{:S(2)}, u32[]{:S(2)}) collective-permute-start(bf16[1408,512]{1,0:T(8,128)(2,1)} %collective-permute-done.27.refs_1_), channel_id=1, source_target_pairs={{1,2},{2,3},{5,6},{6,7},{9,10},{10,11},{13,14},{14,15},{17,18},{18... | collective-permute-start | bytes 4325384 | tf_op jit(solution)/shard_map/ppermute | solution.py:259
  413.5 91.9 %collective-permute-start.30 = (bf16[1408,512]{1,0:T(8,128)(2,1)}, bf16[1408,512]{1,0:T(8,128)(2,1)S(1)}, u32[]{:S(2)}, u32[]{:S(2)}) collective-permute-start(bf16[1408,512]{1,0:T(8,128)(2,1)} %collective-permute-done.28.refs_2_), channel_id=1, source_target_pairs={{1,0},{2,1},{5,4},{6,5},{9,8},{10,9},{13,12},{14,13},{17,16},{18,1... | collective-permute-start | bytes 4325384 | tf_op jit(solution)/shard_map/ppermute | solution.py:260
  443.6 62.5 %collective-permute-start.23 = (bf16[1408,512]{1,0:T(8,128)(2,1)}, bf16[1408,512]{1,0:T(8,128)(2,1)S(1)}, u32[]{:S(2)}, u32[]{:S(2)}) collective-permute-start(bf16[1408,512]{1,0:T(8,128)(2,1)} %collective-permute-done.21.refs_1_), channel_id=1, source_target_pairs={{1,2},{2,3},{5,6},{6,7},{9,10},{10,11},{13,14},{14,15},{17,18},{18... | collective-permute-start | bytes 4325384 | tf_op jit(solution)/shard_map/ppermute | solution.py:259
  444.4 91.9 %collective-permute-start.24 = (bf16[1408,512]{1,0:T(8,128)(2,1)S(1)}, bf16[1408,512]{1,0:T(8,128)(2,1)S(1)}, u32[]{:S(2)}, u32[]{:S(2)}) collective-permute-start(bf16[1408,512]{1,0:T(8,128)(2,1)S(1)} %collective-permute-done.22.refs_2_), channel_id=1, source_target_pairs={{1,0},{2,1},{5,4},{6,5},{9,8},{10,9},{13,12},{14,13},{17,16},{18,1... | collective-permute-start | bytes 4325384 | tf_op jit(solution)/shard_map/ppermute | solution.py:260
  474.5 62.5 %collective-permute-start.17 = (bf16[1408,512]{1,0:T(8,128)(2,1)S(1)}, bf16[1408,512]{1,0:T(8,128)(2,1)S(1)}, u32[]{:S(2)}, u32[]{:S(2)}) collective-permute-start(bf16[1408,512]{1,0:T(8,128)(2,1)S(1)} %collective-permute-done.15.refs_1_), channel_id=1, source_target_pairs={{1,2},{2,3},{5,6},{6,7},{9,10},{10,11},{13,14},{14,15},{17,18},{18... | collective-permute-start | bytes 4325384 | tf_op jit(solution)/shard_map/ppermute | solution.py:259
  475.3 92.0 %collective-permute-start.18 = (bf16[1408,512]{1,0:T(8,128)(2,1)S(1)}, bf16[1408,512]{1,0:T(8,128)(2,1)}, u32[]{:S(2)}, u32[]{:S(2)}) collective-permute-start(bf16[1408,512]{1,0:T(8,128)(2,1)S(1)} %collective-permute-done.16.refs_2_), channel_id=1, source_target_pairs={{1,0},{2,1},{5,4},{6,5},{9,8},{10,9},{13,12},{14,13},{17,16},{18,1... | collective-permute-start | bytes 4325384 | tf_op jit(solution)/shard_map/ppermute | solution.py:260
  505.4 62.6 %collective-permute-start.55 = (bf16[1408,512]{1,0:T(8,128)(2,1)S(1)}, bf16[1408,512]{1,0:T(8,128)(2,1)S(1)}, u32[]{:S(2)}, u32[]{:S(2)}) collective-permute-start(bf16[1408,512]{1,0:T(8,128)(2,1)S(1)} %collective-permute-done.53.refs_3_), channel_id=1, source_target_pairs={{2,3},{6,7},{10,11},{14,15},{18,19},{22,23},{26,27},{30,31}} | collective-permute-start | bytes 4325384 | tf_op jit(solution)/shard_map/ppermute | solution.py:259
  506.2 91.9 %collective-permute-start.56 = (bf16[1408,512]{1,0:T(8,128)(2,1)S(1)}, bf16[1408,512]{1,0:T(8,128)(2,1)S(1)}, u32[]{:S(2)}, u32[]{:S(2)}) collective-permute-start(bf16[1408,512]{1,0:T(8,128)(2,1)S(1)} %collective-permute-done.54.refs_4_), channel_id=1, source_target_pairs={{1,0},{5,4},{9,8},{13,12},{17,16},{21,20},{25,24},{29,28}} | collective-permute-start | bytes 4325384 | tf_op jit(solution)/shard_map/ppermute | solution.py:260
  536.3 62.9 %collective-permute-start.49 = (bf16[1408,512]{1,0:T(8,128)(2,1)S(1)}, bf16[1408,512]{1,0:T(8,128)(2,1)S(1)}, u32[]{:S(2)}, u32[]{:S(2)}) collective-permute-start(bf16[1408,512]{1,0:T(8,128)(2,1)S(1)} %collective-permute-done.47.refs_3_), channel_id=1, source_target_pairs={{2,3},{6,7},{10,11},{14,15},{18,19},{22,23},{26,27},{30,31}} | collective-permute-start | bytes 4325384 | tf_op jit(solution)/shard_map/ppermute | solution.py:259
  537.1 91.9 %collective-permute-start.50 = (bf16[1408,512]{1,0:T(8,128)(2,1)S(1)}, bf16[1408,512]{1,0:T(8,128)(2,1)S(1)}, u32[]{:S(2)}, u32[]{:S(2)}) collective-permute-start(bf16[1408,512]{1,0:T(8,128)(2,1)S(1)} %collective-permute-done.48.refs_4_), channel_id=1, source_target_pairs={{1,0},{5,4},{9,8},{13,12},{17,16},{21,20},{25,24},{29,28}} | collective-permute-start | bytes 4325384 | tf_op jit(solution)/shard_map/ppermute | solution.py:260
  567.3 62.5 %collective-permute-start.43 = (bf16[1408,512]{1,0:T(8,128)(2,1)S(1)}, bf16[1408,512]{1,0:T(8,128)(2,1)S(1)}, u32[]{:S(2)}, u32[]{:S(2)}) collective-permute-start(bf16[1408,512]{1,0:T(8,128)(2,1)S(1)} %collective-permute-done.41.refs_3_), channel_id=1, source_target_pairs={{2,3},{6,7},{10,11},{14,15},{18,19},{22,23},{26,27},{30,31}} | collective-permute-start | bytes 4325384 | tf_op jit(solution)/shard_map/ppermute | solution.py:259
  568.1 91.8 %collective-permute-start.44 = (bf16[1408,512]{1,0:T(8,128)(2,1)S(1)}, bf16[1408,512]{1,0:T(8,128)(2,1)S(1)}, u32[]{:S(2)}, u32[]{:S(2)}) collective-permute-start(bf16[1408,512]{1,0:T(8,128)(2,1)S(1)} %collective-permute-done.42.refs_4_), channel_id=1, source_target_pairs={{1,0},{5,4},{9,8},{13,12},{17,16},{21,20},{25,24},{29,28}} | collective-permute-start | bytes 4325384 | tf_op jit(solution)/shard_map/ppermute | solution.py:260
  598.1 62.5 %collective-permute-start.37 = (bf16[1408,512]{1,0:T(8,128)(2,1)S(1)}, bf16[1408,512]{1,0:T(8,128)(2,1)S(1)}, u32[]{:S(2)}, u32[]{:S(2)}) collective-permute-start(bf16[1408,512]{1,0:T(8,128)(2,1)S(1)} %collective-permute-done.35.refs_3_), channel_id=1, source_target_pairs={{2,3},{6,7},{10,11},{14,15},{18,19},{22,23},{26,27},{30,31}} | collective-permute-start | bytes 4325384 | tf_op jit(solution)/shard_map/ppermute | solution.py:259
  599.3 91.5 %collective-permute-start.38 = (bf16[1408,512]{1,0:T(8,128)(2,1)S(1)}, bf16[1408,512]{1,0:T(8,128)(2,1)S(1)}, u32[]{:S(2)}, u32[]{:S(2)}) collective-permute-start(bf16[1408,512]{1,0:T(8,128)(2,1)S(1)} %collective-permute-done.36.refs_4_), channel_id=1, source_target_pairs={{1,0},{5,4},{9,8},{13,12},{17,16},{21,20},{25,24},{29,28}} | collective-permute-start | bytes 4325384 | tf_op jit(solution)/shard_map/ppermute | solution.py:260
  629.0 62.5 %collective-permute-start.31 = (bf16[1408,512]{1,0:T(8,128)(2,1)S(1)}, bf16[1408,512]{1,0:T(8,128)(2,1)S(1)}, u32[]{:S(2)}, u32[]{:S(2)}) collective-permute-start(bf16[1408,512]{1,0:T(8,128)(2,1)S(1)} %collective-permute-done.29.refs_3_), channel_id=1, source_target_pairs={{2,3},{6,7},{10,11},{14,15},{18,19},{22,23},{26,27},{30,31}} | collective-permute-start | bytes 4325384 | tf_op jit(solution)/shard_map/ppermute | solution.py:259
  629.8 91.9 %collective-permute-start.32 = (bf16[1408,512]{1,0:T(8,128)(2,1)S(1)}, bf16[1408,512]{1,0:T(8,128)(2,1)S(1)}, u32[]{:S(2)}, u32[]{:S(2)}) collective-permute-start(bf16[1408,512]{1,0:T(8,128)(2,1)S(1)} %collective-permute-done.30.refs_4_), channel_id=1, source_target_pairs={{1,0},{5,4},{9,8},{13,12},{17,16},{21,20},{25,24},{29,28}} | collective-permute-start | bytes 4325384 | tf_op jit(solution)/shard_map/ppermute | solution.py:260
  659.9 63.6 %collective-permute-start.25 = (bf16[1408,512]{1,0:T(8,128)(2,1)S(1)}, bf16[1408,512]{1,0:T(8,128)(2,1)S(1)}, u32[]{:S(2)}, u32[]{:S(2)}) collective-permute-start(bf16[1408,512]{1,0:T(8,128)(2,1)S(1)} %collective-permute-done.23.refs_3_), channel_id=1, source_target_pairs={{2,3},{6,7},{10,11},{14,15},{18,19},{22,23},{26,27},{30,31}} | collective-permute-start | bytes 4325384 | tf_op jit(solution)/shard_map/ppermute | solution.py:259
  660.7 91.9 %collective-permute-start.26 = (bf16[1408,512]{1,0:T(8,128)(2,1)S(1)}, bf16[1408,512]{1,0:T(8,128)(2,1)S(1)}, u32[]{:S(2)}, u32[]{:S(2)}) collective-permute-start(bf16[1408,512]{1,0:T(8,128)(2,1)S(1)} %collective-permute-done.24.refs_4_), channel_id=1, source_target_pairs={{1,0},{5,4},{9,8},{13,12},{17,16},{21,20},{25,24},{29,28}} | collective-permute-start | bytes 4325384 | tf_op jit(solution)/shard_map/ppermute | solution.py:260
  690.8 63.1 %collective-permute-start.19 = (bf16[1408,512]{1,0:T(8,128)(2,1)S(1)}, bf16[1408,512]{1,0:T(8,128)(2,1)S(1)}, u32[]{:S(2)}, u32[]{:S(2)}) collective-permute-start(bf16[1408,512]{1,0:T(8,128)(2,1)S(1)} %collective-permute-done.17.refs_3_), channel_id=1, source_target_pairs={{2,3},{6,7},{10,11},{14,15},{18,19},{22,23},{26,27},{30,31}} | collective-permute-start | bytes 4325384 | tf_op jit(solution)/shard_map/ppermute | solution.py:259
  691.6 107.9 %collective-permute-start.20 = (bf16[1408,512]{1,0:T(8,128)(2,1)}, bf16[1408,512]{1,0:T(8,128)(2,1)}, u32[]{:S(2)}, u32[]{:S(2)}) collective-permute-start(bf16[1408,512]{1,0:T(8,128)(2,1)} %collective-permute-done.18.refs_4_), channel_id=1, source_target_pairs={{1,0},{5,4},{9,8},{13,12},{17,16},{21,20},{25,24},{29,28}} | collective-permute-start | bytes 4325384 | tf_op jit(solution)/shard_map/ppermute | solution.py:260
  721.7 83.0 %collective-permute-start.13 = (bf16[1280,512]{1,0:T(8,128)(2,1)}, bf16[1280,512]{1,0:T(8,128)(2,1)}, u32[]{:S(2)}, u32[]{:S(2)}) collective-permute-start(bf16[1280,512]{1,0:T(8,128)(2,1)} %collective-permute-done.11.refs_3_), channel_id=1, source_target_pairs={{2,3},{6,7},{10,11},{14,15},{18,19},{22,23},{26,27},{30,31}} | collective-permute-start | bytes 3932168 | tf_op jit(solution)/shard_map/ppermute | solution.py:259
  723.5 85.2 %collective-permute-start.14 = (bf16[1280,512]{1,0:T(8,128)(2,1)}, bf16[1280,512]{1,0:T(8,128)(2,1)}, u32[]{:S(2)}, u32[]{:S(2)}) collective-permute-start(bf16[1280,512]{1,0:T(8,128)(2,1)} %collective-permute-done.12.refs_4_), channel_id=1, source_target_pairs={{1,0},{5,4},{9,8},{13,12},{17,16},{21,20},{25,24},{29,28}} | collective-permute-start | bytes 3932168 | tf_op jit(solution)/shard_map/ppermute | solution.py:260
  752.6 61.0 %collective-permute-start.7 = (bf16[128,512]{1,0:T(8,128)(2,1)}, bf16[128,512]{1,0:T(8,128)(2,1)}, u32[]{:S(2)}, u32[]{:S(2)}) collective-permute-start(bf16[128,512]{1,0:T(8,128)(2,1)} %collective-permute-done.5.refs_3_), channel_id=1, source_target_pairs={{2,3},{6,7},{10,11},{14,15},{18,19},{22,23},{26,27},{30,31}} | collective-permute-start | bytes 393224 | tf_op jit(solution)/shard_map/ppermute | solution.py:259
  753.9 59.7 %collective-permute-start.8 = (bf16[128,512]{1,0:T(8,128)(2,1)}, bf16[128,512]{1,0:T(8,128)(2,1)}, u32[]{:S(2)}, u32[]{:S(2)}) collective-permute-start(bf16[128,512]{1,0:T(8,128)(2,1)} %collective-permute-done.6.refs_4_), channel_id=1, source_target_pairs={{1,0},{5,4},{9,8},{13,12},{17,16},{21,20},{25,24},{29,28}} | collective-permute-start | bytes 393224 | tf_op jit(solution)/shard_map/ppermute | solution.py:260
  (47 other events, 5208.2 us)
